TPU v7x, 32 devices: a whole 2x2x4 slice. The times are simulated.
32 devices in a mesh: rack: 4 (over x, core), chip: 8 (over z, y).
Axes of the slice: x: 2, y: 2, z: 4, core: 2. Of those that a mesh axis runs over, the one named last changes fastest.
Arguments:
- points: float32 [64, 4, 32, 256], P(('rack', 'chip')), may hold values from -6 to 6
- counts: int32 [64, 256], P(('rack', 'chip')), may hold values from 1 to 32
- cells: int32 [64, 256], P(('rack', 'chip')), may hold values from 0 to 2047, as said below
- pfn_weight: float32 [9, 64], replicated, may hold values from -2 to 2
- pfn_gain: float32 [64], replicated, may hold values from 0.5 to 1.5
- pfn_bias: float32 [64], replicated, may hold values from -3 to 3
- conv_weight: float32 [4, 9, 4096], replicated, may hold values from -0.25 to 0.25
- bn_gain: float32 [4, 64], replicated, may hold values from 0.5 to 1.5
- bn_bias: float32 [4, 64], replicated, may hold values from -3 to 3
- cotangent: float32 [64, 64, 4, 128], P(('rack', 'chip')), may hold values from -0.006 to 0.006
Outputs:
- features: float32 [64, 64, 4, 128], P(('rack', 'chip'))
- conv_grads: float32 [4, 9, 4096], replicated
- norm_grads: float32 [2, 4, 64], replicated
- pillar_grad: float32 [64, 64, 256], P(('rack', 'chip'))
Inputs may be any that keep to these rules, and one draw needn't show every extreme that they name: `cells`: within one sweep no two pillars share a cell.
All inputs are finite; a program needn't handle non-finite values.
Results may differ from a plain program's by a relative error of at most 0.0003.
Values sent between devices are 32-bit elements; how exact they have to be, the bound alone decides.
A program may use at most 128 MiB of HBM per device.

v0:
```python
import functools

import jax
import jax.numpy as jnp
from jax import lax
from jax.experimental import pallas as pl
from jax.experimental.pallas import tpu as pltpu
from jax.sharding import PartitionSpec as P

LAYERS = 4
EPS = 1e-05
F32 = jnp.float32
BF16 = jnp.bfloat16
NN = (((1,), (0,)), ((), ()))
NT = (((1,), (1,)), ((), ()))
LOWEST = -3e38


class Peer:
    def __init__(self, rack, chip, index):
        self.rack, self.chip, self.index = rack, chip, index


def dot(a, b, dims=NN):
    return lax.dot_general(a, b, dims, preferred_element_type=F32)


def split(x):
    hi = x.astype(BF16)
    lo = (x - hi.astype(F32)).astype(BF16)
    return hi, lo


def kernel(
    dims,
    points,
    counts,
    cells,
    pw_s,
    pw,
    pfn_gain,
    pfn_bias,
    w4,
    bn_gain,
    bn_bias,
    cot,
    feat,
    out_g,
    norms,
    pgrad,
    xs,
    gs,
    wfs,
    wbs,
    wb0s,
    onehot,
    par,
    cot_s,
    grads,
    bm,
    mx,
    sq,
    xh,
    yy,
    gz_s,
    st0,
    st,
    rs,
    rbuf,
    st_send,
    st_recv,
    rs_send,
    rs_recv,
    ag_send,
    ag_recv,
):
    n_rack, n_chip, sweeps, maxp, gh, gw, pill, ch, owners = dims
    n = n_rack * n_chip
    h2, w2 = gh // 2, gw // 2
    plane = h2 * w2
    pix = sweeps * plane
    rows_per = ch // owners
    kdim = 9 * ch
    my_rack, my_chip = lax.axis_index("rack"), lax.axis_index("chip")
    me = my_rack * n_chip + my_chip

    def device(t):
        if isinstance(t, Peer):
            return {"rack": t.rack, "chip": t.chip}
        return {"rack": lax.div(t, n_chip), "chip": lax.rem(t, n_chip)}

    def far(k):
        dr, dc = divmod(k, n_chip)
        return -min(dc, n_chip - dc) - min(dr, n_rack - dr)

    def peers(body):
        if n <= 32:
            for k in sorted(range(1, n), key=far):
                dr, dc = divmod(k, n_chip)
                rack = lax.rem(my_rack + dr, n_rack) if dr else my_rack
                chip = lax.rem(my_chip + dc, n_chip) if dc else my_chip
                body(Peer(rack, chip, rack * n_chip + chip))
            return

        def step(k, carry):
            body(lax.rem(me + k, n))
            return carry

        lax.fori_loop(1, n, step, 0)

    barrier = pltpu.get_barrier_semaphore()
    peers(
        lambda t: pl.semaphore_signal(
            barrier, inc=1, device_id=device(t), device_id_type=pl.DeviceIdType.MESH
        )
    )

    def send_row(buf, rnd, row):
        buf[rnd, me] = row

        def go(t):
            pltpu.make_async_remote_copy(
                src_ref=buf.at[rnd, me],
                dst_ref=buf.at[rnd, me],
                send_sem=st_send.at[rnd],
                recv_sem=st_recv.at[rnd],
                device_id=device(t),
                device_id_type=pl.DeviceIdType.MESH,
            ).start()

        peers(go)

    def wait_row(buf, rnd):
        most = buf.at[rnd, pl.ds(0, n - 1)]
        pltpu.make_async_copy(most, most, st_recv.at[rnd]).wait()
        return buf[rnd]

    def send_parts(layer):
        def go(t):
            def copy():
                pltpu.make_async_remote_copy(
                    src_ref=rs.at[layer, t.index if isinstance(t, Peer) else t],
                    dst_ref=rbuf.at[layer, me],
                    send_sem=rs_send.at[layer],
                    recv_sem=rs_recv.at[layer],
                    device_id=device(t),
                    device_id_type=pl.DeviceIdType.MESH,
                ).start()

            if owners == n:
                copy()
            else:
                pl.when(t < owners)(copy)

        peers(go)

    def when_owner(body):
        if owners == n:
            body()
        else:
            pl.when(me < owners)(body)

    def add_parts(layer):
        def body():
            most = rbuf.at[layer, pl.ds(0, n - 1)]
            pltpu.make_async_copy(most, most, rs_recv.at[layer]).wait()
            rbuf[layer, me] = rs[layer, me]
            grads[layer, me] = jnp.sum(rbuf[layer], axis=0)

            def go(t):
                pltpu.make_async_remote_copy(
                    src_ref=grads.at[layer, me],
                    dst_ref=grads.at[layer, me],
                    send_sem=ag_send.at[layer],
                    recv_sem=ag_recv.at[layer],
                    device_id=device(t),
                    device_id_type=pl.DeviceIdType.MESH,
                ).start()

            peers(go)

        when_owner(body)

    slot = lax.broadcasted_iota(jnp.int32, (maxp, pill), 0)
    lane = lax.broadcasted_iota(jnp.int32, (1, 2 * ch), 1)
    per_sweep = []
    spots = []
    totals = [jnp.zeros((1, 1), F32)] * 9
    n_loc = jnp.zeros((1, 1), F32)
    for s in range(sweeps):
        valid = slot < counts[s : s + 1, :]
        mask = valid.astype(F32)
        cnt = counts[s : s + 1, :].astype(F32)
        sums = [jnp.sum(points[s, f] * mask, axis=0, keepdims=True) for f in range(4)]
        cents = [sums[f] / cnt for f in range(3)]
        cell = cells[s : s + 1, :]
        row = lax.shift_right_logical(cell, gw.bit_length() - 1)
        col = cell & (gw - 1)
        col_pos = col.astype(F32) * (2.0 / gw) - 1.0
        row_pos = row.astype(F32) * (2.0 / gh) - 1.0
        feats = sums + [sums[f] - cnt * cents[f] for f in range(3)]
        feats += [sums[0] - cnt * col_pos, sums[1] - cnt * row_pos]
        totals = [t + jnp.sum(f, axis=1, keepdims=True) for t, f in zip(totals, feats)]
        n_loc = n_loc + jnp.sum(cnt, axis=1, keepdims=True)
        per_sweep.append(cents + [col_pos, row_pos])
        spot = ((row & 1) * 2 + (col & 1)) * plane
        spot = spot + lax.shift_right_logical(row, 1) * w2 + lax.shift_right_logical(col, 1)
        spots.append(spot)
    par[...] = jnp.zeros(par.shape, F32)
    par[0:9, 0:ch] = pw[...]
    par[9:10, 0:ch] = pfn_gain[...]
    par[10:11, 0:ch] = pfn_bias[...]
    par[11 : 11 + LAYERS, 0:ch] = bn_gain[...]
    par[11 + LAYERS : 11 + 2 * LAYERS, 0:ch] = bn_bias[...]
    par_cols = par[...].T
    pw_cols = par_cols[0:ch, 0:9]
    gain_c, bias_c = par_cols[0:ch, 9:10], par_cols[0:ch, 10:11]
    bn_cols = par_cols[0:ch, 11 : 11 + 2 * LAYERS]
    m_loc = jnp.zeros((ch, 1), F32)
    for f in range(9):
        m_loc = m_loc + pw_cols[:, f : f + 1] * totals[f]
    m_loc = m_loc / n_loc
    for s in range(sweeps):
        base = -m_loc
        for f in range(5):
            base = base - pw_cols[:, f + 4 : f + 5] * per_sweep[s][f]
        bm[s] = base

    def one_channel(c, carry):
        wx = pw_s[0, c] + pw_s[4, c] + pw_s[7, c]
        wy = pw_s[1, c] + pw_s[5, c] + pw_s[8, c]
        wz = pw_s[2, c] + pw_s[6, c]
        wr = pw_s[3, c]
        total = jnp.zeros((8, pill), F32)
        for s in range(sweeps):
            most = jnp.full((8, pill), LOWEST, F32)
            shift = bm[s, pl.ds(c, 1), :]
            have = counts[s : s + 1, :]
            for k in range(maxp // 8):
                part = pl.ds(8 * k, 8)
                ids = lax.broadcasted_iota(jnp.int32, (8, pill), 0) + 8 * k
                ok = ids < have
                h = points[s, 0, part, :] * wx + points[s, 1, part, :] * wy
                h = h + points[s, 2, part, :] * wz + points[s, 3, part, :] * wr + shift
                most = jnp.maximum(most, jnp.where(ok, h, LOWEST))
                h = jnp.where(ok, h, 0.0)
                total = total + h * h
            mx[s, c] = most
        folded = total[:, 0:128]
        for t in range(1, pill // 128):
            folded = folded + total[:, t * 128 : (t + 1) * 128]
        sq[c] = folded
        return carry

    lax.fori_loop(0, ch, one_channel, 0)
    both = jnp.concatenate([jnp.broadcast_to(m_loc, (ch, 128)), jnp.sum(sq[...], axis=1)], axis=0)
    turned = both.T
    row = jnp.where(lane < ch, turned[0:1, :], jnp.sum(turned, axis=0, keepdims=True))
    row = jnp.concatenate([row, jnp.broadcast_to(n_loc, (1, 2 * ch))], axis=1)

    pl.semaphore_wait(barrier, n - 1)
    send_row(st0, 0, row)

    def forward_weights(layer):
        w = [w4[layer, t * ch : (t + 1) * ch, :] for t in range(9)]
        hi, lo = split(jnp.concatenate(w, axis=1))
        wfs[layer, 0:ch, :] = hi
        wfs[layer, ch : 2 * ch, :] = lo

    def backward_weights(layer):
        hi, lo = split(w4[layer].T)
        wbs[layer - 1, 0:ch, :] = hi
        wbs[layer - 1, ch : 2 * ch, :] = lo

    def first_backward_weights():
        w = w4[0].T
        zero = jnp.zeros((ch, ch), F32)
        tap_of = {(0, 0): 1, (1, 0): 2, (1, 1): 0}
        for k in range(4):
            line = []
            for j in range(4):
                a, b = tap_of.get((k // 2, j // 2)), tap_of.get((k % 2, j % 2))
                t = None if a is None or b is None else 3 * a + b
                line.append(zero if t is None else w[:, t * ch : (t + 1) * ch])
            hi, lo = split(jnp.concatenate(line, axis=1))
            wb0s[k * ch : (k + 1) * ch, :] = hi
            wb0s[(4 + k) * ch : (5 + k) * ch, :] = lo

    for s in range(sweeps):
        for k in range(4):
            ids = lax.broadcasted_iota(jnp.int32, (plane, pill), 0) + k * plane
            onehot[s, k * plane : (k + 1) * plane, :] = (ids == spots[s]).astype(F32).astype(BF16)
    for s in range(sweeps):
        bm[s] = jnp.max(mx[s], axis=1)
    forward_weights(0)

    def columns(row):
        turned = jnp.broadcast_to(row, (8, 2 * ch)).T
        return turned[0:ch, 0:1], turned[ch : 2 * ch, 0:1]

    got = wait_row(st0, 0)
    n_all = jnp.sum(got[:, :, 2 * ch :], axis=0)
    rows = got[:, :, 0 : 2 * ch]
    weighted = got[:, :, 2 * ch :]
    means = jnp.sum(rows * weighted, axis=0) / n_all
    dev = rows - means[None]
    spread = jnp.sum(dev * dev * weighted, axis=0)
    second = (jnp.sum(rows, axis=0) + pltpu.roll(spread, ch, axis=1)) / n_all
    mean_c, inv_c = columns(jnp.where(lane < ch, means, lax.rsqrt(second + EPS)))
    scale_c = gain_c * inv_c
    shift_c = scale_c * (m_loc - mean_c) + bias_c

    ids = lax.broadcasted_iota(jnp.int32, (1, pix), 1)
    col_id = ids & (w2 - 1)
    row_id = lax.shift_right_logical(ids, w2.bit_length() - 1) & (h2 - 1)

    def moved(x, dr, dc):
        ok = None
        if dc == -1:
            ok = col_id >= 1
        elif dc == 1:
            ok = col_id < w2 - 1
        if dr == -1:
            rok = row_id >= 1
            ok = rok if ok is None else ok & rok
        elif dr == 1:
            rok = row_id < h2 - 1
            ok = rok if ok is None else ok & rok
        if ok is None:
            return x
        return jnp.where(ok, pltpu.roll(x, (-(dr * w2 + dc)) % pix, axis=1), 0.0)

    planes = [[], [], [], []]
    for s in range(sweeps):
        pillar = jnp.maximum(bm[s] * scale_c + shift_c, 0.0)
        hi, lo = split(pillar)
        placed = dot(jnp.concatenate([hi, lo], axis=0), onehot[s], NT)
        for k in range(4):
            part = placed[:, k * plane : (k + 1) * plane]
            planes[k].append(part[0:ch] + part[ch : 2 * ch])
    planes = [jnp.concatenate(p, axis=1) for p in planes]
    for a in range(3):
        for b in range(3):
            which = (0 if a == 1 else 2) + (0 if b == 1 else 1)
            tap = moved(planes[which], -1 if a == 0 else 0, -1 if b == 0 else 0)
            hi, lo = split(tap)
            at = pl.ds((3 * a + b) * ch, ch)
            xs[0, 0, at, :] = hi
            xs[0, 1, at, :] = lo

    entries_loc = float(pix)
    entries = float(pix * n)

    def fold(x):
        out = x[:, 0:128]
        for t in range(1, pix // 128):
            out = out + x[:, t * 128 : (t + 1) * 128]
        return out

    def slope(y):
        sig = jax.nn.sigmoid(y)
        return sig * (1.0 + y * (1.0 - sig))

    for layer in range(LAYERS):
        big = dot(wfs[layer], xs[layer, 0])
        z = big[0:ch] + big[ch : 2 * ch] + dot(wfs[layer, 0:ch, :], xs[layer, 1])
        sums = fold(z)
        m_loc = jnp.sum(sums, axis=1, keepdims=True) / entries_loc
        d = z - m_loc
        turned = jnp.concatenate([sums, fold(d * d)], axis=0).T
        row = jnp.sum(turned, axis=0, keepdims=True)
        row = jnp.where(lane < ch, row / entries_loc, row)
        send_row(st, layer + 1, row)
        if layer == 0:
            first_backward_weights()
        else:
            backward_weights(layer)
            yy[layer - 1] = slope(yy[layer - 1])
        if layer + 1 < LAYERS:
            forward_weights(layer + 1)
        else:
            for s in range(sweeps):
                for r in range(h2):
                    at = s * plane + r * w2
                    cot_s[:, at : at + w2] = cot[s, :, r, :]
        rows = wait_row(st, layer + 1)
        total = jnp.sum(rows, axis=0)
        means = total / float(n)
        dev = rows - means[None]
        spread = jnp.sum(dev * dev, axis=0) * entries_loc
        second = (total + pltpu.roll(spread, ch, axis=1)) / entries
        row = jnp.where(lane < ch, means, lax.rsqrt(second + EPS))
        mean_c, inv_c = columns(row)
        normed = (z - mean_c) * inv_c
        y = bn_cols[:, layer : layer + 1] * normed
        y = y + bn_cols[:, LAYERS + layer : LAYERS + layer + 1]
        xh[layer] = normed
        sq[layer, :, :] = jnp.broadcast_to(row, (8, 2 * ch))
        sig = jax.nn.sigmoid(y)
        act = y * sig
        yy[layer] = y if layer + 1 < LAYERS else sig * (1.0 + y * (1.0 - sig))
        if layer + 1 < LAYERS:
            for a in range(3):
                for b in range(3):
                    hi, lo = split(moved(act, a - 1, b - 1))
                    at = pl.ds((3 * a + b) * ch, ch)
                    xs[layer + 1, 0, at, :] = hi
                    xs[layer + 1, 1, at, :] = lo

    def weight_grad(layer):
        both = gz_s[...]
        big = dot(both, xs[layer, 0], NT)
        dw = big[0:ch] + big[ch : 2 * ch] + dot(both[0:ch], xs[layer, 1], NT)
        for j in range(owners):
            rs[layer, j] = dw[j * rows_per : (j + 1) * rows_per, :]
        send_parts(layer)

    u = cot_s[...]
    for layer in range(LAYERS - 1, -1, -1):
        normed = xh[layer]
        gy = u * yy[layer]
        turned = jnp.concatenate([fold(gy), fold(gy * normed)], axis=0).T
        rnd = 2 * LAYERS - layer
        send_row(st, rnd, jnp.sum(turned, axis=0, keepdims=True))
        if layer == LAYERS - 1:
            for s in range(sweeps):
                for r in range(h2):
                    at = s * plane + r * w2
                    feat[s, :, r, :] = act[:, at : at + w2]
        if layer < LAYERS - 1:
            weight_grad(layer + 1)
        if layer < LAYERS - 2:
            add_parts(layer + 2)
        row = jnp.sum(wait_row(st, rnd), axis=0)
        norms[0, layer : layer + 1, :] = row[:, ch : 2 * ch]
        norms[1, layer : layer + 1, :] = row[:, 0:ch]
        dy_c, dyx_c = columns(row / entries)
        inv_c = columns(sq[layer, 0:1, :])[1]
        gz = (bn_cols[:, layer : layer + 1] * inv_c) * (gy - dy_c - normed * dyx_c)
        hi, lo = split(gz)
        gz_s[0:ch, :] = hi
        gz_s[ch : 2 * ch, :] = lo
        if layer > 0:
            for a in range(3):
                for b in range(3):
                    hi, lo = split(moved(gz, 1 - a, 1 - b))
                    at = pl.ds((3 * a + b) * ch, ch)
                    gs[0, at, :] = hi
                    gs[1, at, :] = lo
            big = dot(wbs[layer - 1], gs[0])
            u = big[0:ch] + big[ch : 2 * ch] + dot(wbs[layer - 1, 0:ch, :], gs[1])
    weight_grad(0)
    add_parts(1)
    for dr in range(2):
        for dc in range(2):
            hi, lo = split(moved(gz, dr, dc))
            at = pl.ds((2 * dr + dc) * ch, ch)
            gs[0, at, :] = hi
            gs[1, at, :] = lo
    big = dot(wb0s[...], gs[0, 0 : 4 * ch, :])
    u0 = big[0 : 4 * ch] + big[4 * ch :] + dot(wb0s[0 : 4 * ch, :], gs[1, 0 : 4 * ch, :])
    for s in range(sweeps):
        total = None
        for k in range(4):
            hi, lo = split(u0[k * ch : (k + 1) * ch, s * plane : (s + 1) * plane])
            part = dot(
                jnp.concatenate([hi, lo], axis=0), onehot[s, k * plane : (k + 1) * plane, :]
            )
            total = part if total is None else total + part
        pgrad[s] = total[0:ch] + total[ch : 2 * ch]
    add_parts(0)

    for layer in range(LAYERS - 1, -1, -1):
        others = grads.at[layer, pl.ds(0, owners - 1)]
        if owners == n:
            pltpu.make_async_copy(others, others, ag_recv.at[layer]).wait()
        else:
            all_of = grads.at[layer]

            @pl.when(me < owners)
            def _():
                pltpu.make_async_copy(others, others, ag_recv.at[layer]).wait()

            @pl.when(me >= owners)
            def _():
                pltpu.make_async_copy(all_of, all_of, ag_recv.at[layer]).wait()

        whole = grads[layer].reshape(ch, kdim)
        for t in range(9):
            out_g[layer, t] = whole[:, t * ch : (t + 1) * ch]

    for rnd in range(2 * LAYERS + 1):
        most = (st0.at[0] if rnd == 0 else st.at[rnd]).at[pl.ds(0, n - 1)]
        pltpu.make_async_copy(most, most, st_send.at[rnd]).wait()
    for layer in range(LAYERS):
        others = rs.at[layer, pl.ds(0, owners - 1)]
        sent = rbuf.at[layer, pl.ds(0, n - 1)]
        if owners == n:
            pltpu.make_async_copy(others, others, rs_send.at[layer]).wait()
            pltpu.make_async_copy(sent, sent, ag_send.at[layer]).wait()
        else:
            all_of = rs.at[layer]

            @pl.when(me < owners)
            def _():
                pltpu.make_async_copy(others, others, rs_send.at[layer]).wait()
                pltpu.make_async_copy(sent, sent, ag_send.at[layer]).wait()

            @pl.when(me >= owners)
            def _():
                pltpu.make_async_copy(all_of, all_of, rs_send.at[layer]).wait()


def per_device(
    n_rack,
    n_chip,
    points,
    counts,
    cells,
    pfn_weight,
    pfn_gain,
    pfn_bias,
    conv_weight,
    bn_gain,
    bn_bias,
    cotangent,
):
    sweeps, _, maxp, pill = points.shape
    ch = pfn_weight.shape[1]
    h2, w2 = cotangent.shape[2:]
    gh, gw = 2 * h2, 2 * w2
    n = n_rack * n_chip
    owners = min(n, ch)
    rows_per = ch // owners
    pix = sweeps * h2 * w2
    kdim = 9 * ch
    dims = (n_rack, n_chip, sweeps, maxp, gh, gw, pill, ch, owners)
    vmem = pl.BlockSpec(memory_space=pltpu.VMEM)
    smem = pl.BlockSpec(memory_space=pltpu.SMEM)
    feat, out_g, norms, pgrad = pl.pallas_call(
        functools.partial(kernel, dims),
        out_shape=(
            jax.ShapeDtypeStruct((sweeps, ch, h2, w2), F32),
            jax.ShapeDtypeStruct((LAYERS, 9, ch, ch), F32),
            jax.ShapeDtypeStruct((2, LAYERS, ch), F32),
            jax.ShapeDtypeStruct((sweeps, ch, pill), F32),
        ),
        in_specs=[vmem, vmem, vmem, smem] + [vmem] * 7,
        out_specs=(vmem, vmem, vmem, vmem),
        scratch_shapes=[
            pltpu.VMEM((LAYERS, 2, kdim, pix), BF16),
            pltpu.VMEM((2, kdim, pix), BF16),
            pltpu.VMEM((LAYERS, 2 * ch, kdim), BF16),
            pltpu.VMEM((LAYERS - 1, 2 * ch, kdim), BF16),
            pltpu.VMEM((8 * ch, 4 * ch), BF16),
            pltpu.VMEM((sweeps, gh * gw, pill), BF16),
            pltpu.VMEM((32, 128), F32),
            pltpu.VMEM((ch, pix), F32),
            pltpu.VMEM((LAYERS, owners, rows_per, kdim), F32),
            pltpu.VMEM((sweeps, ch, pill), F32),
            pltpu.VMEM((sweeps, ch, 8, pill), F32),
            pltpu.VMEM((ch, 8, 128), F32),
            pltpu.VMEM((LAYERS, ch, pix), F32),
            pltpu.VMEM((LAYERS, ch, pix), F32),
            pltpu.VMEM((2 * ch, pix), BF16),
            pltpu.VMEM((1, n, 1, 4 * ch), F32),
            pltpu.VMEM((2 * LAYERS + 1, n, 1, 2 * ch), F32),
            pltpu.VMEM((LAYERS, owners, rows_per, kdim), F32),
            pltpu.VMEM((LAYERS, n, rows_per, kdim), F32),
            pltpu.SemaphoreType.DMA((2 * LAYERS + 1,)),
            pltpu.SemaphoreType.DMA((2 * LAYERS + 1,)),
            pltpu.SemaphoreType.DMA((LAYERS,)),
            pltpu.SemaphoreType.DMA((LAYERS,)),
            pltpu.SemaphoreType.DMA((LAYERS,)),
            pltpu.SemaphoreType.DMA((LAYERS,)),
        ],
        compiler_params=pltpu.CompilerParams(
            collective_id=0, has_side_effects=True, vmem_limit_bytes=60 * 1024 * 1024
        ),
    )(
        points,
        counts,
        cells,
        pfn_weight,
        pfn_weight,
        pfn_gain.reshape(1, ch),
        pfn_bias.reshape(1, ch),
        conv_weight.reshape(LAYERS, kdim, ch),
        bn_gain,
        bn_bias,
        cotangent,
    )
    return (feat, out_g.reshape(LAYERS, 9, ch * ch), norms, pgrad)


def solution(mesh):
    both = ("rack", "chip")
    return jax.shard_map(
        functools.partial(per_device, mesh.shape["rack"], mesh.shape["chip"]),
        mesh=mesh,
        in_specs=(
            P(both, None, None, None),
            P(both, None),
            P(both, None),
            P(),
            P(),
            P(),
            P(),
            P(),
            P(),
            P(both, None, None, None),
        ),
        out_specs=(
            P(both, None, None, None),
            P(),
            P(),
            P(both, None, None),
        ),
        check_vma=False,
    )
```

profile of v0, /device:TPU:0, one launch (start us, length us, event | category | flops | bytes accessed | tf_op | source)
XLA Modules:
  0.0 87.5 jit_solution(12281726996186627643)
XLA Ops:
  0.6 1.4 %copy.16 = f32[4,9,4096]{2,1,0:T(8,128)S(1)} copy(f32[4,9,4096]{2,0,1:T(4,128)} %param.16) | data formatting | bytes 1179648 | tf_op args[6]
  2.1 1.5 %reshape.22.w4 = f32[4,576,64]{2,1,0:T(8,128)} reshape(f32[4,9,4096]{2,1,0:T(8,128)S(1)} %copy.16) | data formatting | bytes 1179648 | tf_op jit(solution)/shard_map/reshape | solution.py:588
  3.5 79.1 %shard_map.129 = (f32[2,64,4,128]{3,2,1,0:T(4,128)}, f32[4,9,64,64]{3,2,1,0:T(8,128)}, f32[2,4,64]{2,1,0:T(4,128)}, f32[2,64,256]{2,1,0:T(8,128)}) custom-call(f32[2,4,32,256]{3,2,1,0:T(8,128)} %points.1, s32[2,256]{1,0:T(2,128)} %counts.1, s32[2,256]{1,0:T(2,128)} %cells.1, f32[9,64]{1,0:T(8,128)} %pw.1, f32[9,64]{1,0:T(8,128)} %pw.1, f32[1,64]{1,0:T(1,128)} %bitcast.4, ...), custom_call_target="tpu_custom_call" | custom-call | tf_op jit(solution)/shard_map/pallas_call | solution.py:540
  82.7 1.7 %reshape.24 = f32[4,9,4096]{2,1,0:T(8,128)S(1)} reshape(f32[4,9,64,64]{3,2,1,0:T(8,128)} %get-tuple-element.9) | data formatting | bytes 1179648 | tf_op jit(solution)/shard_map/reshape | solution.py:593
  84.4 0.0 copy-start
  84.4 0.0 copy-start.2
  84.4 0.0 copy-start.1
  84.4 1.2 %copy.18 = f32[4,9,4096]{2,0,1:T(4,128)} copy(f32[4,9,4096]{2,1,0:T(8,128)S(1)} %reshape.24) | data formatting | bytes 1179648 | tf_op jit(solution)/shard_map/reshape | solution.py:593
  85.6 0.0 copy-done
  85.6 0.7 copy.22
  86.3 0.0 copy-done.2
  86.3 0.6 copy.23
  86.9 0.0 copy-done.1
  86.9 0.7 copy.24
Async XLA Ops:
  84.4 1.2 %copy-start = (f32[2,64,4,128]{3,2,1,0:T(4,128)S(1)}, f32[2,64,4,128]{3,2,1,0:T(4,128)}, u32[]{:S(2)}) copy-start(f32[2,64,4,128]{3,2,1,0:T(4,128)} %get-tuple-element.20) | copy-start | bytes 786436
  84.4 1.9 %copy-start.2 = (f32[2,4,64]{2,1,0:T(4,128)S(1)}, f32[2,4,64]{2,1,0:T(4,128)}, u32[]{:S(2)}) copy-start(f32[2,4,64]{2,1,0:T(4,128)} %get-tuple-element.22) | copy-start | bytes 6148
  84.4 2.5 %copy-start.1 = (f32[2,64,256]{2,1,0:T(8,128)S(1)}, f32[2,64,256]{2,1,0:T(8,128)}, u32[]{:S(2)}) copy-start(f32[2,64,256]{2,1,0:T(8,128)} %get-tuple-element.23) | copy-start | bytes 393220
where the time goes:
time: 87.8 us; the launch traced here: 87.5 us
  Pallas kernels  79.1 us (90%)
  local copies, waits for them, and re-layouts  7.77 us (9%)
    pallas_call x1, Pallas kernels, per_device(): pl.pallas_call(functools.partial(kernel, dims), out_shape=(jax.ShapeDtype...  79.1 us
    unnamed x10, local copies, waits for them, and re-layouts  3.39 us
    reshape x2, local copies, waits for them, and re-layouts, per_device(): return (feat, out_g.reshape(LAYERS, 9, ch * ch), norms, pgrad)  2.89 us

commit v1 on v0

v1 whole, which is shorter than its diff:
```python
import functools

import jax
import jax.numpy as jnp
from jax import lax
from jax.experimental import pallas as pl
from jax.experimental.pallas import tpu as pltpu
from jax.sharding import PartitionSpec as P

LAYERS = 4
LINEAR = (0, 1)
EPS = 1e-05
F32 = jnp.float32
BF16 = jnp.bfloat16
NN = (((1,), (0,)), ((), ()))
NT = (((1,), (1,)), ((), ()))
LOWEST = -3e38


class Peer:
    def __init__(self, rack, chip, index):
        self.rack, self.chip, self.index = rack, chip, index


def dot(a, b, dims=NN):
    return lax.dot_general(a, b, dims, preferred_element_type=F32)


def split(x):
    hi = x.astype(BF16)
    lo = (x - hi.astype(F32)).astype(BF16)
    return hi, lo


def kernel(
    dims,
    points_h,
    counts_h,
    cells_h,
    pw_h,
    pfn_gain_h,
    pfn_bias_h,
    w4_h,
    bn_gain_h,
    bn_bias_h,
    cot_h,
    feat,
    out_g,
    norms,
    pgrad,
    points,
    counts,
    cells,
    pw,
    pw_s,
    pfn_gain,
    pfn_bias,
    w4,
    bn_gain,
    bn_bias,
    cot,
    xs,
    gs,
    hs,
    res,
    wn,
    wfs,
    wbs,
    wb0s,
    g4,
    onehot,
    par,
    cot_s,
    grads,
    bm,
    mx,
    sq,
    xh,
    yy,
    st0,
    st,
    rs,
    rbuf,
    rx,
    rxbuf,
    in_sem,
    st_send,
    st_recv,
    rs_send,
    rs_recv,
    rx_send,
    rx_recv,
    ag_send,
    ag_recv,
):
    n_rack, n_chip, sweeps, maxp, gh, gw, pill, ch, owners = dims
    n = n_rack * n_chip
    h2, w2 = gh // 2, gw // 2
    plane = h2 * w2
    pix = sweeps * plane
    ch3 = 3 * ch
    my_rack, my_chip = lax.axis_index("rack"), lax.axis_index("chip")
    me = my_rack * n_chip + my_chip

    fetches = [
        (points_h, points),
        (counts_h, counts),
        (cells_h, cells),
        (pw_h, pw),
        (pw_h, pw_s),
        (pfn_gain_h, pfn_gain),
        (pfn_bias_h, pfn_bias),
        (bn_gain_h, bn_gain),
        (bn_bias_h, bn_bias),
        (w4_h, w4),
        (cot_h, cot),
    ]
    fetches = [pltpu.make_async_copy(a, b, in_sem.at[i]) for i, (a, b) in enumerate(fetches)]

    def device(t):
        if isinstance(t, Peer):
            return {"rack": t.rack, "chip": t.chip}
        return {"rack": lax.div(t, n_chip), "chip": lax.rem(t, n_chip)}

    def far(k):
        dr, dc = divmod(k, n_chip)
        return -min(dc, n_chip - dc) - min(dr, n_rack - dr)

    def peers(body):
        if n <= 32:
            for k in sorted(range(1, n), key=far):
                dr, dc = divmod(k, n_chip)
                rack = lax.rem(my_rack + dr, n_rack) if dr else my_rack
                chip = lax.rem(my_chip + dc, n_chip) if dc else my_chip
                body(Peer(rack, chip, rack * n_chip + chip))
            return

        def step(k, carry):
            body(lax.rem(me + k, n))
            return carry

        lax.fori_loop(1, n, step, 0)

    for f in fetches:
        f.start()
    barrier = pltpu.get_barrier_semaphore()
    peers(
        lambda t: pl.semaphore_signal(
            barrier, inc=1, device_id=device(t), device_id_type=pl.DeviceIdType.MESH
        )
    )

    def remote(src, dst, send, recv, t):
        pltpu.make_async_remote_copy(
            src_ref=src,
            dst_ref=dst,
            send_sem=send,
            recv_sem=recv,
            device_id=device(t),
            device_id_type=pl.DeviceIdType.MESH,
        ).start()

    def landed(ref, sem):
        pltpu.make_async_copy(ref, ref, sem).wait()

    def send_row(buf, rnd, row):
        buf[rnd, me] = row
        mine = buf.at[rnd, me]
        peers(lambda t: remote(mine, mine, st_send.at[rnd], st_recv.at[rnd], t))

    def wait_row(buf, rnd):
        landed(buf.at[rnd, pl.ds(0, n - 1)], st_recv.at[rnd])
        return buf[rnd]

    def send_parts(src, dst, send, recv):
        def go(t):
            index = t.index if isinstance(t, Peer) else t

            def copy():
                remote(src.at[index], dst.at[me], send, recv, t)

            if owners == n:
                copy()
            else:
                pl.when(t.index < owners if isinstance(t, Peer) else t < owners)(copy)

        peers(go)

    def when_owner(body):
        if owners == n:
            body()
        else:
            pl.when(me < owners)(body)

    lane = lax.broadcasted_iota(jnp.int32, (1, 2 * ch), 1)

    def add_parts(layer):
        def body():
            landed(rbuf.at[layer, pl.ds(0, n - 1)], rs_recv.at[layer])
            rbuf[layer, me] = rs[layer, me]
            total = jnp.sum(rbuf[layer], axis=0)
            if layer in LINEAR:
                at = LINEAR.index(layer)
                landed(rxbuf.at[at, pl.ds(0, n - 1)], rx_recv.at[at])
                rxbuf[at, me] = rx[at, me]
                extra = jnp.sum(rxbuf[at], axis=0)

                def mine(row):
                    even = jnp.sum(jnp.where(lane == 2 * me, row, 0.0), axis=1, keepdims=True)
                    odd = jnp.sum(jnp.where(lane == 2 * me + 1, row, 0.0), axis=1, keepdims=True)
                    return jnp.where(lane < ch, even, odd)

                sums = sigmas[layer]
                inv = pltpu.roll(sq[layer, 0:1, :], ch, axis=1)
                gain = par[11 + layer : 12 + layer, :]
                c_dy = mine(sums / entries)
                c_dx = mine(pltpu.roll(sums, ch, axis=1) / entries)
                total = total - c_dy * extra[9:18] - c_dx * extra[0:9]
                total = mine(gain * inv) * total
            grads[layer, me] = total
            out = grads.at[layer, me]
            peers(lambda t: remote(out, out, ag_send.at[layer], ag_recv.at[layer], t))

        when_owner(body)

    for f in fetches[0:5]:
        f.wait()
    slot = lax.broadcasted_iota(jnp.int32, (maxp, pill), 0)
    per_sweep = []
    spots = []
    totals = [jnp.zeros((1, 1), F32)] * 9
    n_loc = jnp.zeros((1, 1), F32)
    for s in range(sweeps):
        valid = slot < counts[s : s + 1, :]
        mask = valid.astype(F32)
        cnt = counts[s : s + 1, :].astype(F32)
        sums = [jnp.sum(points[s, f] * mask, axis=0, keepdims=True) for f in range(4)]
        cents = [sums[f] / cnt for f in range(3)]
        cell = cells[s : s + 1, :]
        row = lax.shift_right_logical(cell, gw.bit_length() - 1)
        col = cell & (gw - 1)
        col_pos = col.astype(F32) * (2.0 / gw) - 1.0
        row_pos = row.astype(F32) * (2.0 / gh) - 1.0
        feats = sums + [sums[f] - cnt * cents[f] for f in range(3)]
        feats += [sums[0] - cnt * col_pos, sums[1] - cnt * row_pos]
        totals = [t + jnp.sum(f, axis=1, keepdims=True) for t, f in zip(totals, feats)]
        n_loc = n_loc + jnp.sum(cnt, axis=1, keepdims=True)
        per_sweep.append(cents + [col_pos, row_pos])
        spot = ((row & 1) * 2 + (col & 1)) * plane
        spot = spot + lax.shift_right_logical(row, 1) * w2 + lax.shift_right_logical(col, 1)
        spots.append(spot)
    for f in fetches[5:9]:
        f.wait()
    par[...] = jnp.zeros(par.shape, F32)
    par[0:9, 0:ch] = pw[...]
    par[9:10, 0:ch] = pfn_gain[...]
    par[10:11, 0:ch] = pfn_bias[...]
    par[11 : 11 + LAYERS, 0:ch] = bn_gain[...]
    par[11 + LAYERS : 11 + 2 * LAYERS, 0:ch] = bn_bias[...]
    par_cols = par[...].T
    pw_cols = par_cols[0:ch, 0:9]
    gain_c, bias_c = par_cols[0:ch, 9:10], par_cols[0:ch, 10:11]
    bn_cols = par_cols[0:ch, 11 : 11 + 2 * LAYERS]
    m_loc = jnp.zeros((ch, 1), F32)
    for f in range(9):
        m_loc = m_loc + pw_cols[:, f : f + 1] * totals[f]
    m_loc = m_loc / n_loc
    for s in range(sweeps):
        base = -m_loc
        for f in range(5):
            base = base - pw_cols[:, f + 4 : f + 5] * per_sweep[s][f]
        bm[s] = base

    def one_channel(c, carry):
        wx = pw_s[0, c] + pw_s[4, c] + pw_s[7, c]
        wy = pw_s[1, c] + pw_s[5, c] + pw_s[8, c]
        wz = pw_s[2, c] + pw_s[6, c]
        wr = pw_s[3, c]
        total = jnp.zeros((8, pill), F32)
        for s in range(sweeps):
            most = jnp.full((8, pill), LOWEST, F32)
            shift_by = bm[s, pl.ds(c, 1), :]
            have = counts[s : s + 1, :]
            for k in range(maxp // 8):
                part = pl.ds(8 * k, 8)
                ids = lax.broadcasted_iota(jnp.int32, (8, pill), 0) + 8 * k
                ok = ids < have
                h = points[s, 0, part, :] * wx + points[s, 1, part, :] * wy
                h = h + points[s, 2, part, :] * wz + points[s, 3, part, :] * wr + shift_by
                most = jnp.maximum(most, jnp.where(ok, h, LOWEST))
                h = jnp.where(ok, h, 0.0)
                total = total + h * h
            mx[s, c] = most
        folded = total[:, 0:128]
        for t in range(1, pill // 128):
            folded = folded + total[:, t * 128 : (t + 1) * 128]
        sq[c] = folded
        return carry

    lax.fori_loop(0, ch, one_channel, 0)
    both = jnp.concatenate([jnp.broadcast_to(m_loc, (ch, 128)), jnp.sum(sq[...], axis=1)], axis=0)
    turned = both.T
    row = jnp.where(lane < ch, turned[0:1, :], jnp.sum(turned, axis=0, keepdims=True))
    row = jnp.concatenate([row, jnp.broadcast_to(n_loc, (1, 2 * ch))], axis=1)

    pl.semaphore_wait(barrier, n - 1)
    send_row(st0, 0, row)

    col = lax.broadcasted_iota(jnp.int32, (1, w2), 1)
    tiles = pix // w2

    def tile(x, t):
        return x[:, t * w2 : (t + 1) * w2]

    def shift(x, d):
        if d == 0:
            return x
        ok = col >= -d if d < 0 else col < w2 - d
        return jnp.concatenate(
            [jnp.where(ok, pltpu.roll(tile(x, t), (-d) % w2, axis=1), 0.0) for t in range(tiles)],
            axis=1,
        )

    def down(x, d):
        parts = []
        for s in range(sweeps):
            for r in range(h2):
                inside = 0 <= r + d < h2
                t = s * h2 + r + d
                parts.append(tile(x, t) if inside else jnp.zeros((x.shape[0], w2), x.dtype))
        return jnp.concatenate(parts, axis=1)

    def stack_rows(at, per_tap):
        for a, (x, d) in enumerate(per_tap):
            for h in range(2):
                xs[at, h, a * ch : (a + 1) * ch, :] = down(x[h], d) if d else x[h]

    def stack_cols(ref, step, x):
        for b in range(3):
            for h, part in enumerate(split(shift(x, 1 - b))):
                ref[h * step + b * ch : h * step + (b + 1) * ch, :] = part

    def natural(layer):
        half = ch // 2
        for b in range(3):
            v = [w4[3 * a + b, :, layer, :] for a in range(3)]
            for k in range(2):
                v3 = [x[:, k * ch : (k + 1) * ch] for x in v]
                rows = pl.ds(b * ch + k, half, stride=2)
                wn[0, rows, :] = jnp.concatenate(v3[0:2], axis=1)
                wn[1, rows, :] = jnp.concatenate([v3[2], v3[2]], axis=1)
        return jnp.concatenate([wn[0], wn[1, :, 0:ch]], axis=1)

    def weights(layer):
        w = natural(layer)
        hi, lo = split(w)
        if layer == 0:
            for h, part in enumerate((hi, lo)):
                wfs[0, h * 2 * ch : (h * 2 + 1) * ch, :] = part[0:ch]
                wfs[0, (h * 2 + 1) * ch : (h * 2 + 2) * ch, :] = part[2 * ch : ch3]
                wfs[0, (4 + h) * ch : (5 + h) * ch, :] = part[ch : 2 * ch]
            first_backward_weights(w.T)
        else:
            wfs[layer, 0:ch3, :] = hi
            wfs[layer, ch3 : 2 * ch3, :] = lo
            hi, lo = split(w.T)
            wbs[layer - 1, 0:ch3, :] = hi
            wbs[layer - 1, ch3 : 2 * ch3, :] = lo

    def first_backward_weights(w):
        zero = jnp.zeros((ch, ch), F32)
        tap_of = {(0, 0): 1, (1, 0): 2, (1, 1): 0}
        for k in range(4):
            line = []
            for j in range(4):
                a, b = tap_of.get((k // 2, j // 2)), tap_of.get((k % 2, j % 2))
                none = a is None or b is None
                line.append(zero if none else w[a * ch : (a + 1) * ch, b * ch : (b + 1) * ch])
            hi, lo = split(jnp.concatenate(line, axis=1))
            wb0s[k * ch : (k + 1) * ch, :] = hi
            wb0s[(4 + k) * ch : (5 + k) * ch, :] = lo

    for s in range(sweeps):
        for k in range(4):
            ids = lax.broadcasted_iota(jnp.int32, (plane, pill), 0) + k * plane
            onehot[s, k * plane : (k + 1) * plane, :] = (ids == spots[s]).astype(F32).astype(BF16)
    for s in range(sweeps):
        bm[s] = jnp.max(mx[s], axis=1)
    for f in fetches[9:11]:
        f.wait()
    weights(0)
    inside = lax.broadcasted_iota(jnp.int32, (16, pix), 0)
    cols = lax.broadcasted_iota(jnp.int32, (16, pix), 1) & (w2 - 1)
    ones = ((inside == 0) & (cols < w2 - 1)) | (inside == 1) | ((inside == 2) & (cols >= 1))
    hs[ch3 : ch3 + 16, :] = ones.astype(F32).astype(BF16)
    hs[2 * ch3 + 16 : 2 * ch3 + 32, :] = jnp.zeros((16, pix), BF16)

    def columns(row):
        turned = jnp.broadcast_to(row, (8, 2 * ch)).T
        return turned[0:ch, 0:1], turned[ch : 2 * ch, 0:1]

    got = wait_row(st0, 0)
    n_all = jnp.sum(got[:, :, 2 * ch :], axis=0)
    rows = got[:, :, 0 : 2 * ch]
    weighted = got[:, :, 2 * ch :]
    means = jnp.sum(rows * weighted, axis=0) / n_all
    dev = rows - means[None]
    spread = jnp.sum(dev * dev * weighted, axis=0)
    second = (jnp.sum(rows, axis=0) + pltpu.roll(spread, ch, axis=1)) / n_all
    mean_c, inv_c = columns(jnp.where(lane < ch, means, lax.rsqrt(second + EPS)))
    scale_c = gain_c * inv_c
    shift_c = scale_c * (m_loc - mean_c) + bias_c

    planes = [[], [], [], []]
    for s in range(sweeps):
        pillar = jnp.maximum(bm[s] * scale_c + shift_c, 0.0)
        hi, lo = split(pillar)
        placed = dot(jnp.concatenate([hi, lo], axis=0), onehot[s], NT)
        for k in range(4):
            part = placed[:, k * plane : (k + 1) * plane]
            planes[k].append(part[0:ch] + part[ch : 2 * ch])
    planes = [split(jnp.concatenate(p, axis=1)) for p in planes]
    for k in range(2):
        stack_rows(k, [(planes[2 + k], -1), (planes[k], 0), (planes[2 + k], 0)])

    entries_loc = float(pix)
    entries = float(pix * n)

    def fold(x):
        out = x[:, 0:128]
        for t in range(1, pix // 128):
            out = out + x[:, t * 128 : (t + 1) * 128]
        return out

    def parts3(w, k, at):
        big = dot(w, xs[at, 0])
        return big[0:k] + big[k : 2 * k] + dot(w[0:k], xs[at, 1])

    def convolve(layer):
        if layer == 0:
            y = parts3(wfs[0, 0 : 4 * ch, :], 2 * ch, 1)
            return parts3(wfs[0, 4 * ch : 6 * ch, :], ch, 0) + y[ch : 2 * ch] + shift(y[0:ch], -1)
        y = parts3(wfs[layer], ch3, layer + 1)
        return y[ch : 2 * ch] + shift(y[0:ch], -1) + shift(y[2 * ch : ch3], 1)

    def correlate(both, k, at):
        big = dot(both, xs[at, 0], NT)
        return big[0:k] + big[k : 2 * k] + dot(both[0:k], xs[at, 1], NT)

    def pairs(store):
        half = ch // 2
        for b in range(3):
            for a in range(3):
                at = slice((a % 2) * ch, (a % 2 + 1) * ch)
                even = res[a // 2, pl.ds(b * ch, half, stride=2), :]
                odd = res[a // 2, pl.ds(b * ch + 1, half, stride=2), :]
                store(3 * a + b, jnp.concatenate([even[:, at], odd[:, at]], axis=1))

    def keep(at, x):
        res[0, at, :] = x[:, 0 : 2 * ch]
        res[1, at, 0:ch] = x[:, 2 * ch : ch3]

    def send_grad(ref, layer):
        if layer == 0:
            some = jnp.concatenate([ref[0 : 2 * ch, :], ref[ch3 : ch3 + 2 * ch, :]], axis=0)
            odd = correlate(some, 2 * ch, 1)
            some = jnp.concatenate([ref[ch : 2 * ch, :], ref[ch3 + ch : ch3 + 2 * ch, :]], axis=0)
            keep(slice(0, ch), odd[0:ch])
            keep(slice(ch, 2 * ch), correlate(some, ch, 0))
            keep(slice(2 * ch, ch3), odd[ch : 2 * ch])
        else:
            keep(slice(0, ch3), correlate(ref[...], ch3, layer + 1))

        def store(t, line):
            rs[layer, :, t, :] = line

        pairs(store)
        send_parts(rs.at[layer], rbuf.at[layer], rs_send.at[layer], rs_recv.at[layer])

    def send_extra(layer):
        at = LINEAR.index(layer)
        k = ch3 + 16
        stack_cols(hs, k, xh[layer])
        if layer == 0:
            even, odd = correlate(hs[...], k, 0), correlate(hs[...], k, 1)
            keep(slice(0, ch), odd[0:ch])
            keep(slice(ch, 2 * ch), even[ch : 2 * ch])
            keep(slice(2 * ch, ch3), odd[ch : 2 * ch])
            window = [odd[ch3 : ch3 + 1], even[ch3 + 1 : ch3 + 2], odd[ch3 + 1 : ch3 + 2]]
        else:
            both = correlate(hs[...], k, layer + 1)
            keep(slice(0, ch3), both[0:ch3])
            window = [both[ch3 + b : ch3 + b + 1] for b in range(3)]

        def store(t, line):
            rx[at, :, t, :] = line

        pairs(store)
        for b in range(3):
            for a in range(3):
                one = window[b][:, a * ch : (a + 1) * ch]
                line = jnp.concatenate([one, one], axis=1)
                rx[at, :, 9 + 3 * a + b, :] = jnp.broadcast_to(line, (owners, 2 * ch))
        send_parts(rx.at[at], rxbuf.at[at], rx_send.at[at], rx_recv.at[at])

    def finish(layer):
        scale, off, inv, by = affine[layer]
        d = xh[layer]
        y = scale * d + off
        xh[layer] = inv * (d - by)
        sig = jax.nn.sigmoid(y)
        yy[layer] = sig * (1.0 + y * (1.0 - sig))

    affine = []
    sigmas = {}
    act = None
    for layer in range(LAYERS):
        z = convolve(layer)
        sums = fold(z)
        m_loc = jnp.sum(sums, axis=1, keepdims=True) / entries_loc
        d = z - m_loc
        turned = jnp.concatenate([sums, fold(d * d)], axis=0).T
        row = jnp.sum(turned, axis=0, keepdims=True)
        row = jnp.where(lane < ch, row / entries_loc, row)
        send_row(st, layer + 1, row)
        xh[layer] = d
        if layer + 1 < LAYERS:
            weights(layer + 1)
        else:
            for s in range(sweeps):
                for r in range(h2):
                    at = s * plane + r * w2
                    cot_s[:, at : at + w2] = cot[s, :, r, :]
        if layer > 0:
            finish(layer - 1)
            if layer - 1 in LINEAR:
                send_extra(layer - 1)
        rows = wait_row(st, layer + 1)
        total = jnp.sum(rows, axis=0)
        means = total / float(n)
        dev = rows - means[None]
        spread = jnp.sum(dev * dev, axis=0) * entries_loc
        second = (total + pltpu.roll(spread, ch, axis=1)) / entries
        row = jnp.where(lane < ch, means, lax.rsqrt(second + EPS))
        mean_c, inv_c = columns(row)
        sq[layer, :, :] = jnp.broadcast_to(row, (8, 2 * ch))
        by = mean_c - m_loc
        scale = bn_cols[:, layer : layer + 1] * inv_c
        off = bn_cols[:, LAYERS + layer : LAYERS + layer + 1] - scale * by
        affine.append((scale, off, inv_c, by))
        y = scale * xh[layer] + off
        act = y * jax.nn.sigmoid(y)
        if layer + 1 < LAYERS:
            hi_lo = split(act)
            stack_rows(layer + 2, [(hi_lo, -1), (hi_lo, 0), (hi_lo, 1)])
        else:
            finish(layer)

    def backward(layer):
        w = wbs[layer - 1]
        big = dot(w, gs[0:ch3, :])
        v = big[0:ch3] + big[ch3 : 2 * ch3] + dot(w[0:ch3], gs[ch3 : 2 * ch3, :])
        return v[ch : 2 * ch] + down(v[0:ch], 1) + down(v[2 * ch : ch3], -1)

    u = cot_s[...]
    for layer in range(LAYERS - 1, -1, -1):
        gy = u * yy[layer]
        turned = jnp.concatenate([fold(gy), fold(gy * xh[layer])], axis=0).T
        rnd = 2 * LAYERS - layer
        send_row(st, rnd, jnp.sum(turned, axis=0, keepdims=True))
        if layer == LAYERS - 1:
            for s in range(sweeps):
                for r in range(h2):
                    at = s * plane + r * w2
                    feat[s, :, r, :] = act[:, at : at + w2]
        if layer in LINEAR:
            stack_cols(hs, ch3, gy)
            send_grad(hs.at[0 : 2 * ch3, :], layer)
        if layer + 1 < LAYERS and layer + 1 not in LINEAR:
            send_grad(gs, layer + 1)
        for done in range(layer + 1, LAYERS):
            if done == layer + (1 if done in LINEAR else 2):
                add_parts(done)
        row = jnp.sum(wait_row(st, rnd), axis=0)
        sigmas[layer] = row
        norms[0, layer : layer + 1, :] = row[:, ch : 2 * ch]
        norms[1, layer : layer + 1, :] = row[:, 0:ch]
        dy_c, dyx_c = columns(row / entries)
        gz = affine[layer][0] * (gy - dy_c - xh[layer] * dyx_c)
        if layer > 0:
            stack_cols(gs, ch3, gz)
            u = backward(layer)
    for dr in range(2):
        for dc in range(2):
            hi, lo = split(shift(down(gz, dr), dc))
            at = pl.ds((2 * dr + dc) * ch, ch)
            g4[0, at, :] = hi
            g4[1, at, :] = lo
    big = dot(wb0s[...], g4[0])
    u0 = big[0 : 4 * ch] + big[4 * ch :] + dot(wb0s[0 : 4 * ch, :], g4[1])
    for s in range(sweeps):
        total = None
        for k in range(4):
            hi, lo = split(u0[k * ch : (k + 1) * ch, s * plane : (s + 1) * plane])
            part = dot(
                jnp.concatenate([hi, lo], axis=0), onehot[s, k * plane : (k + 1) * plane, :]
            )
            total = part if total is None else total + part
        pgrad[s] = total[0:ch] + total[ch : 2 * ch]
    add_parts(0)

    def by_role(mine, theirs):
        if owners == n:
            mine()
        else:
            pl.when(me < owners)(mine)
            pl.when(me >= owners)(theirs)

    for layer in range(LAYERS - 1, -1, -1):
        others = grads.at[layer, pl.ds(0, owners - 1)]
        by_role(
            lambda: landed(others, ag_recv.at[layer]),
            lambda: landed(grads.at[layer], ag_recv.at[layer]),
        )
        for t in range(9):
            out_g[t, :, layer, :] = grads[layer, :, t, :]

    for rnd in range(2 * LAYERS + 1):
        landed((st0.at[0] if rnd == 0 else st.at[rnd]).at[pl.ds(0, n - 1)], st_send.at[rnd])
    for layer in range(LAYERS):
        by_role(
            lambda: landed(rs.at[layer, pl.ds(0, owners - 1)], rs_send.at[layer]),
            lambda: landed(rs.at[layer], rs_send.at[layer]),
        )
        when_owner(lambda: landed(rbuf.at[layer, pl.ds(0, n - 1)], ag_send.at[layer]))
    for at in range(len(LINEAR)):
        by_role(
            lambda: landed(rx.at[at, pl.ds(0, owners - 1)], rx_send.at[at]),
            lambda: landed(rx.at[at], rx_send.at[at]),
        )


def write_out(a, b, c, d, a_h, b_h, c_h, d_h, sem):
    pairs = [(a, a_h), (b, b_h), (c, c_h), (d, d_h)]
    copies = [pltpu.make_async_copy(x, y, sem.at[i]) for i, (x, y) in enumerate(pairs)]
    for x in copies:
        x.start()
    for x in copies:
        x.wait()


def per_device(
    n_rack,
    n_chip,
    points,
    counts,
    cells,
    pfn_weight,
    pfn_gain,
    pfn_bias,
    conv_weight,
    bn_gain,
    bn_bias,
    cotangent,
):
    sweeps, _, maxp, pill = points.shape
    ch = pfn_weight.shape[1]
    h2, w2 = cotangent.shape[2:]
    gh, gw = 2 * h2, 2 * w2
    n = n_rack * n_chip
    owners = ch // 2
    assert n >= owners and w2 == 128 and 2 * ch == 128
    pix = sweeps * h2 * w2
    ch3 = 3 * ch
    dims = (n_rack, n_chip, sweeps, maxp, gh, gw, pill, ch, owners)
    hbm = pl.BlockSpec(memory_space=pl.ANY)
    vmem = pl.BlockSpec(memory_space=pltpu.VMEM)
    extra = len(LINEAR)
    w4 = conv_weight.reshape(LAYERS, 9, owners, 2 * ch).transpose(1, 2, 0, 3)
    dma = pltpu.SemaphoreType.DMA
    outs = pl.pallas_call(
        functools.partial(kernel, dims),
        out_shape=(
            pltpu.VMEM((sweeps, ch, h2, w2), F32),
            pltpu.VMEM((9, owners, LAYERS, 2 * ch), F32),
            pltpu.VMEM((2, LAYERS, ch), F32),
            pltpu.VMEM((sweeps, ch, pill), F32),
        ),
        in_specs=[hbm] * 10,
        out_specs=(vmem,) * 4,
        scratch_shapes=[
            pltpu.VMEM((sweeps, 4, maxp, pill), F32),
            pltpu.VMEM((sweeps, pill), jnp.int32),
            pltpu.VMEM((sweeps, pill), jnp.int32),
            pltpu.VMEM((9, ch), F32),
            pltpu.SMEM((9, ch), F32),
            pltpu.VMEM((1, ch), F32),
            pltpu.VMEM((1, ch), F32),
            pltpu.VMEM((9, owners, LAYERS, 2 * ch), F32),
            pltpu.VMEM((LAYERS, ch), F32),
            pltpu.VMEM((LAYERS, ch), F32),
            pltpu.VMEM((sweeps, ch, h2, w2), F32),
            pltpu.VMEM((LAYERS + 1, 2, ch3, pix), BF16),
            pltpu.VMEM((2 * ch3, pix), BF16),
            pltpu.VMEM((2 * ch3 + 32, pix), BF16),
            pltpu.VMEM((2, ch3, 2 * ch), F32),
            pltpu.VMEM((2, ch3, 2 * ch), F32),
            pltpu.VMEM((LAYERS, 2 * ch3, ch3), BF16),
            pltpu.VMEM((LAYERS - 1, 2 * ch3, ch3), BF16),
            pltpu.VMEM((8 * ch, 4 * ch), BF16),
            pltpu.VMEM((2, 4 * ch, pix), BF16),
            pltpu.VMEM((sweeps, gh * gw, pill), BF16),
            pltpu.VMEM((32, 128), F32),
            pltpu.VMEM((ch, pix), F32),
            pltpu.VMEM((LAYERS, owners, 9, 2 * ch), F32),
            pltpu.VMEM((sweeps, ch, pill), F32),
            pltpu.VMEM((sweeps, ch, 8, pill), F32),
            pltpu.VMEM((ch, 8, 128), F32),
            pltpu.VMEM((LAYERS, ch, pix), F32),
            pltpu.VMEM((LAYERS, ch, pix), F32),
            pltpu.VMEM((1, n, 1, 4 * ch), F32),
            pltpu.VMEM((2 * LAYERS + 1, n, 1, 2 * ch), F32),
            pltpu.VMEM((LAYERS, owners, 9, 2 * ch), F32),
            pltpu.VMEM((LAYERS, n, 9, 2 * ch), F32),
            pltpu.VMEM((extra, owners, 18, 2 * ch), F32),
            pltpu.VMEM((extra, n, 18, 2 * ch), F32),
            dma((11,)),
            dma((2 * LAYERS + 1,)),
            dma((2 * LAYERS + 1,)),
            dma((LAYERS,)),
            dma((LAYERS,)),
            dma((extra,)),
            dma((extra,)),
            dma((LAYERS,)),
            dma((LAYERS,)),
        ],
        compiler_params=pltpu.CompilerParams(
            collective_id=0, has_side_effects=True, vmem_limit_bytes=56 * 1024 * 1024
        ),
    )(
        points,
        counts,
        cells,
        pfn_weight,
        pfn_gain.reshape(1, ch),
        pfn_bias.reshape(1, ch),
        w4,
        bn_gain,
        bn_bias,
        cotangent,
    )
    feat, out_g, norms, pgrad = pl.pallas_call(
        write_out,
        out_shape=tuple(jax.ShapeDtypeStruct(x.shape, x.dtype) for x in outs),
        in_specs=[vmem] * 4,
        out_specs=(hbm,) * 4,
        scratch_shapes=[dma((4,))],
    )(*[pltpu.with_memory_space_constraint(x, pltpu.VMEM) for x in outs])
    grads = out_g.transpose(2, 0, 1, 3).reshape(LAYERS, 9, ch * ch)
    return (feat, grads, norms, pgrad)


def solution(mesh):
    both = ("rack", "chip")
    return jax.shard_map(
        functools.partial(per_device, mesh.shape["rack"], mesh.shape["chip"]),
        mesh=mesh,
        in_specs=(
            P(both, None, None, None),
            P(both, None),
            P(both, None),
            P(),
            P(),
            P(),
            P(),
            P(),
            P(),
            P(both, None, None, None),
        ),
        out_specs=(
            P(both, None, None, None),
            P(),
            P(),
            P(both, None, None),
        ),
        check_vma=False,
    )
```

time: 87.8 us -> 79.1 us (0.901)
  local copies, waits for them, and re-layouts: 7.77 us -> 0 us
    reshape x3 -> x0, local copies, waits for them, and re-layouts: 4.38 us -> none  [the longest x2 2.89 us: per_device(): return (feat, out_g.reshape(LAYERS, 9, ch * ch), norms, pgrad)]
    unnamed x10 -> x0, local copies, waits for them, and re-layouts: 3.39 us -> none
    pallas_call x1 -> x2, Pallas kernels: 79.1 us -> 78.3 us  [the longest x1 77.3 us: per_device(): pl.pallas_call(functools.partial(kernel, dims), out_shape=(pltpu.VMEM((sw...]
where the time goes in v1:
time: 79.1 us; the launch traced here: 78.9 us
  Pallas kernels  78.3 us (99%)
    pallas_call x1, Pallas kernels, per_device(): pl.pallas_call(functools.partial(kernel, dims), out_shape=(pltpu.VMEM((sw...  77.3 us

profile of v1, /device:TPU:0, one launch (start us, length us, event | category | flops | bytes accessed | tf_op | source)
XLA Modules:
  0.0 78.9 jit_solution(13423585784227900556)
XLA Ops:
  0.6 77.3 %shard_map.129 = (f32[2,64,4,128]{3,2,1,0:T(4,128)S(1)}, f32[9,32,4,128]{3,2,1,0:T(4,128)S(1)}, f32[2,4,64]{2,1,0:T(4,128)S(1)}, f32[2,64,256]{2,1,0:T(8,128)S(1)}) custom-call(f32[2,4,32,256]{3,2,1,0:T(8,128)} %points_h.1, s32[2,256]{1,0:T(2,128)} %counts_h.1, s32[2,256]{1,0:T(2,128)} %cells_h.1, f32[9,64]{1,0:T(8,128)} %pw_h.1, f32[1,64]{1,0:T(1,128)} %bitcast.9, ...), custom_call_target="tpu_custom_call" | custom-call | tf_op jit(solution)/shard_map/pallas_call | solution.py:681
  77.9 1.0 %shard_map.130 = (f32[2,64,4,128]{3,2,1,0:T(4,128)}, f32[9,32,4,128]{3,2,1,0:T(4,128)}, f32[2,4,64]{2,1,0:T(4,128)}, f32[2,64,256]{2,1,0:T(8,128)}) custom-call(f32[2,64,4,128]{3,2,1,0:T(4,128)S(1)} %get-tuple-element.12.a, f32[9,32,4,128]{3,2,1,0:T(4,128)S(1)} %get-tuple-element.13.b, f32[2,4,64]{2,1,0:T(4,128)S(1)} %get-tuple-element.14.c, ...), custom_call_target="tpu_custom_call" | custom-call | tf_op jit(solution)/shard_map/pallas_call | solution.py:752

commit v2 on v1

--- a/solution.py
+++ b/solution.py
@@ -80,18 +80,28 @@
     st0,
     st,
     rs,
+    ra,
+    rp,
     rbuf,
     rx,
+    rxa,
+    rxp,
     rxbuf,
     in_sem,
     st_send,
     st_recv,
+    ra_send,
+    ra_recv,
     rs_send,
     rs_recv,
+    rxa_send,
+    rxa_recv,
     rx_send,
     rx_recv,
     ag_send,
     ag_recv,
+    sh_send,
+    sh_recv,
 ):
     n_rack, n_chip, sweeps, maxp, gh, gw, pill, ch, owners = dims
     n = n_rack * n_chip
@@ -101,6 +111,11 @@
     ch3 = 3 * ch
     my_rack, my_chip = lax.axis_index("rack"), lax.axis_index("chip")
     me = my_rack * n_chip + my_chip
+    half, n_same = owners // 2, n // 2
+    core, my_x = lax.rem(my_rack, 2), lax.div(my_rack, 2)
+    place = my_x * n_chip + my_chip
+    slot_of_me = core * half + place
+    twin = Peer(my_rack + 1 - 2 * core, my_chip, 0)
 
     fetches = [
         (points_h, points),
@@ -172,42 +187,80 @@
         landed(buf.at[rnd, pl.ds(0, n - 1)], st_recv.at[rnd])
         return buf[rnd]
 
-    def send_parts(src, dst, send, recv):
+    def same_core(body):
+        if n <= 32:
+            for k in sorted(range(1, n_same), key=far):
+                dx, dc = divmod(k, n_chip)
+                x = lax.rem(my_x + dx, n_rack // 2) if dx else my_x
+                chip = lax.rem(my_chip + dc, n_chip) if dc else my_chip
+                body(Peer(x * 2 + core, chip, x * n_chip + chip))
+            return
+
+        def step(k, carry):
+            at = lax.rem(place + k, n_same)
+            body(Peer(lax.div(at, n_chip) * 2 + core, lax.rem(at, n_chip), at))
+            return carry
+
+        lax.fori_loop(1, n_same, step, 0)
+
+    def to_twin(src, dst, send, recv):
+        remote(src.at[pl.ds((1 - core) * half, half)], dst, send, recv, twin)
+
+    def send_parts(src, came, both, dst, came_sem, send, recv):
+        landed(came, came_sem)
+        both[...] = src[pl.ds(core * half, half)] + came[...]
+
         def go(t):
-            index = t.index if isinstance(t, Peer) else t
-
             def copy():
-                remote(src.at[index], dst.at[me], send, recv, t)
-
-            if owners == n:
+                remote(both.at[t.index], dst.at[place], send, recv, t)
+
+            if half == n_same:
                 copy()
             else:
-                pl.when(t.index < owners if isinstance(t, Peer) else t < owners)(copy)
-
-        peers(go)
+                pl.when(t.index < half)(copy)
+
+        same_core(go)
+
+    def pass_on(layer):
+        send_parts(
+            rs.at[layer],
+            ra.at[layer],
+            rp.at[layer],
+            rbuf.at[layer],
+            ra_recv.at[layer],
+            rs_send.at[layer],
+            rs_recv.at[layer],
+        )
 
     def when_owner(body):
-        if owners == n:
+        if half == n_same:
             body()
         else:
-            pl.when(me < owners)(body)
+            pl.when(place < half)(body)
+
+    def by_role(mine, theirs):
+        if half == n_same:
+            mine()
+        else:
+            pl.when(place < half)(mine)
+            pl.when(place >= half)(theirs)
 
     lane = lax.broadcasted_iota(jnp.int32, (1, 2 * ch), 1)
 
     def add_parts(layer):
         def body():
-            landed(rbuf.at[layer, pl.ds(0, n - 1)], rs_recv.at[layer])
-            rbuf[layer, me] = rs[layer, me]
+            landed(rbuf.at[layer, pl.ds(0, n_same - 1)], rs_recv.at[layer])
+            rbuf[layer, place] = rp[layer, place]
             total = jnp.sum(rbuf[layer], axis=0)
             if layer in LINEAR:
                 at = LINEAR.index(layer)
-                landed(rxbuf.at[at, pl.ds(0, n - 1)], rx_recv.at[at])
-                rxbuf[at, me] = rx[at, me]
+                landed(rxbuf.at[at, pl.ds(0, n_same - 1)], rx_recv.at[at])
+                rxbuf[at, place] = rxp[at, place]
                 extra = jnp.sum(rxbuf[at], axis=0)
 
                 def mine(row):
-                    even = jnp.sum(jnp.where(lane == 2 * me, row, 0.0), axis=1, keepdims=True)
-                    odd = jnp.sum(jnp.where(lane == 2 * me + 1, row, 0.0), axis=1, keepdims=True)
+                    even = jnp.sum(jnp.where(lane == 2 * slot_of_me, row, 0.0), axis=1, keepdims=True)
+                    odd = jnp.sum(jnp.where(lane == 2 * slot_of_me + 1, row, 0.0), axis=1, keepdims=True)
                     return jnp.where(lane < ch, even, odd)
 
                 sums = sigmas[layer]
@@ -217,11 +270,19 @@
                 c_dx = mine(pltpu.roll(sums, ch, axis=1) / entries)
                 total = total - c_dy * extra[9:18] - c_dx * extra[0:9]
                 total = mine(gain * inv) * total
-            grads[layer, me] = total
-            out = grads.at[layer, me]
-            peers(lambda t: remote(out, out, ag_send.at[layer], ag_recv.at[layer], t))
+            grads[layer, slot_of_me] = total
+            out = grads.at[layer, slot_of_me]
+            same_core(lambda t: remote(out, out, ag_send.at[layer], ag_recv.at[layer], t))
 
         when_owner(body)
+
+    def share(layer):
+        by_role(
+            lambda: landed(grads.at[layer, pl.ds(0, half - 1)], ag_recv.at[layer]),
+            lambda: landed(grads.at[layer, pl.ds(0, half)], ag_recv.at[layer]),
+        )
+        ours = grads.at[layer, pl.ds(core * half, half)]
+        remote(ours, ours, sh_send.at[layer], sh_recv.at[layer], twin)
 
     for f in fetches[0:5]:
         f.wait()
@@ -475,7 +536,7 @@
             rs[layer, :, t, :] = line
 
         pairs(store)
-        send_parts(rs.at[layer], rbuf.at[layer], rs_send.at[layer], rs_recv.at[layer])
+        to_twin(rs.at[layer], ra.at[layer], ra_send.at[layer], ra_recv.at[layer])
 
     def send_extra(layer):
         at = LINEAR.index(layer)
@@ -501,7 +562,16 @@
                 one = window[b][:, a * ch : (a + 1) * ch]
                 line = jnp.concatenate([one, one], axis=1)
                 rx[at, :, 9 + 3 * a + b, :] = jnp.broadcast_to(line, (owners, 2 * ch))
-        send_parts(rx.at[at], rxbuf.at[at], rx_send.at[at], rx_recv.at[at])
+        to_twin(rx.at[at], rxa.at[at], rxa_send.at[at], rxa_recv.at[at])
+        send_parts(
+            rx.at[at],
+            rxa.at[at],
+            rxp.at[at],
+            rxbuf.at[at],
+            rxa_recv.at[at],
+            rx_send.at[at],
+            rx_recv.at[at],
+        )
 
     def finish(layer):
         scale, off, inv, by = affine[layer]
@@ -578,9 +648,15 @@
             send_grad(hs.at[0 : 2 * ch3, :], layer)
         if layer + 1 < LAYERS and layer + 1 not in LINEAR:
             send_grad(gs, layer + 1)
-        for done in range(layer + 1, LAYERS):
+        if layer in LINEAR:
+            pass_on(layer)
+        if layer + 1 < LAYERS and layer + 1 not in LINEAR:
+            pass_on(layer + 1)
+        for done in range(LAYERS - 1, layer, -1):
             if done == layer + (1 if done in LINEAR else 2):
                 add_parts(done)
+        if layer == 0:
+            share(LAYERS - 1)
         row = jnp.sum(wait_row(st, rnd), axis=0)
         sigmas[layer] = row
         norms[0, layer : layer + 1, :] = row[:, ch : 2 * ch]
@@ -609,34 +685,29 @@
         pgrad[s] = total[0:ch] + total[ch : 2 * ch]
     add_parts(0)
 
-    def by_role(mine, theirs):
-        if owners == n:
-            mine()
-        else:
-            pl.when(me < owners)(mine)
-            pl.when(me >= owners)(theirs)
+    for layer in range(LAYERS - 2, -1, -1):
+        share(layer)
 
     for layer in range(LAYERS - 1, -1, -1):
-        others = grads.at[layer, pl.ds(0, owners - 1)]
-        by_role(
-            lambda: landed(others, ag_recv.at[layer]),
-            lambda: landed(grads.at[layer], ag_recv.at[layer]),
-        )
+        landed(grads.at[layer, pl.ds(0, half)], sh_recv.at[layer])
         for t in range(9):
             out_g[t, :, layer, :] = grads[layer, :, t, :]
 
     for rnd in range(2 * LAYERS + 1):
         landed((st0.at[0] if rnd == 0 else st.at[rnd]).at[pl.ds(0, n - 1)], st_send.at[rnd])
     for layer in range(LAYERS):
+        landed(ra.at[layer], ra_send.at[layer])
+        landed(grads.at[layer, pl.ds(0, half)], sh_send.at[layer])
         by_role(
-            lambda: landed(rs.at[layer, pl.ds(0, owners - 1)], rs_send.at[layer]),
-            lambda: landed(rs.at[layer], rs_send.at[layer]),
+            lambda: landed(rp.at[layer, pl.ds(0, half - 1)], rs_send.at[layer]),
+            lambda: landed(rp.at[layer], rs_send.at[layer]),
         )
-        when_owner(lambda: landed(rbuf.at[layer, pl.ds(0, n - 1)], ag_send.at[layer]))
+        when_owner(lambda: landed(rbuf.at[layer, pl.ds(0, n_same - 1)], ag_send.at[layer]))
     for at in range(len(LINEAR)):
+        landed(rxa.at[at], rxa_send.at[at])
         by_role(
-            lambda: landed(rx.at[at, pl.ds(0, owners - 1)], rx_send.at[at]),
-            lambda: landed(rx.at[at], rx_send.at[at]),
+            lambda: landed(rxp.at[at, pl.ds(0, half - 1)], rx_send.at[at]),
+            lambda: landed(rxp.at[at], rx_send.at[at]),
         )
 
 
@@ -669,7 +740,7 @@
     gh, gw = 2 * h2, 2 * w2
     n = n_rack * n_chip
     owners = ch // 2
-    assert n >= owners and w2 == 128 and 2 * ch == 128
+    assert n >= owners and n_rack % 2 == 0 and w2 == 128 and 2 * ch == 128
     pix = sweeps * h2 * w2
     ch3 = 3 * ch
     dims = (n_rack, n_chip, sweeps, maxp, gh, gw, pill, ch, owners)
@@ -721,16 +792,26 @@
             pltpu.VMEM((1, n, 1, 4 * ch), F32),
             pltpu.VMEM((2 * LAYERS + 1, n, 1, 2 * ch), F32),
             pltpu.VMEM((LAYERS, owners, 9, 2 * ch), F32),
-            pltpu.VMEM((LAYERS, n, 9, 2 * ch), F32),
+            pltpu.VMEM((LAYERS, owners // 2, 9, 2 * ch), F32),
+            pltpu.VMEM((LAYERS, owners // 2, 9, 2 * ch), F32),
+            pltpu.VMEM((LAYERS, n // 2, 9, 2 * ch), F32),
             pltpu.VMEM((extra, owners, 18, 2 * ch), F32),
-            pltpu.VMEM((extra, n, 18, 2 * ch), F32),
+            pltpu.VMEM((extra, owners // 2, 18, 2 * ch), F32),
+            pltpu.VMEM((extra, owners // 2, 18, 2 * ch), F32),
+            pltpu.VMEM((extra, n // 2, 18, 2 * ch), F32),
             dma((11,)),
             dma((2 * LAYERS + 1,)),
             dma((2 * LAYERS + 1,)),
             dma((LAYERS,)),
             dma((LAYERS,)),
+            dma((LAYERS,)),
+            dma((LAYERS,)),
             dma((extra,)),
             dma((extra,)),
+            dma((extra,)),
+            dma((extra,)),
+            dma((LAYERS,)),
+            dma((LAYERS,)),
             dma((LAYERS,)),
             dma((LAYERS,)),
         ],

time: 79.1 us -> 67.8 us (0.86)
  Pallas kernels: 78.3 us -> 67 us
    pallas_call x1, Pallas kernels: 77.3 us -> 66 us  [per_device(): pl.pallas_call(functools.partial(kernel, dims), out_shape=(pltpu.VMEM((sw...]
where the time goes in v2:
time: 67.8 us; the launch traced here: 67.6 us
  Pallas kernels  67 us (99%)
    pallas_call x1, Pallas kernels, per_device(): pl.pallas_call(functools.partial(kernel, dims), out_shape=(pltpu.VMEM((sw...  66 us

profile of v2, /device:TPU:0, one launch (start us, length us, event | category | flops | bytes accessed | tf_op | source)
XLA Modules:
  0.0 67.6 jit_solution(9610934357362197191)
XLA Ops:
  0.6 66.0 %shard_map.129 = (f32[2,64,4,128]{3,2,1,0:T(4,128)S(1)}, f32[9,32,4,128]{3,2,1,0:T(4,128)S(1)}, f32[2,4,64]{2,1,0:T(4,128)S(1)}, f32[2,64,256]{2,1,0:T(8,128)S(1)}) custom-call(f32[2,4,32,256]{3,2,1,0:T(8,128)} %points_h.1, s32[2,256]{1,0:T(2,128)} %counts_h.1, s32[2,256]{1,0:T(2,128)} %cells_h.1, f32[9,64]{1,0:T(8,128)} %pw_h.1, f32[1,64]{1,0:T(1,128)} %bitcast.9, ...), custom_call_target="tpu_custom_call" | custom-call | tf_op jit(solution)/shard_map/pallas_call | solution.py:752
  66.7 1.0 %shard_map.130 = (f32[2,64,4,128]{3,2,1,0:T(4,128)}, f32[9,32,4,128]{3,2,1,0:T(4,128)}, f32[2,4,64]{2,1,0:T(4,128)}, f32[2,64,256]{2,1,0:T(8,128)}) custom-call(f32[2,64,4,128]{3,2,1,0:T(4,128)S(1)} %get-tuple-element.12.a, f32[9,32,4,128]{3,2,1,0:T(4,128)S(1)} %get-tuple-element.13.b, f32[2,4,64]{2,1,0:T(4,128)S(1)} %get-tuple-element.14.c, ...), custom_call_target="tpu_custom_call" | custom-call | tf_op jit(solution)/shard_map/pallas_call | solution.py:833

commit v3 on v2

--- a/solution.py
+++ b/solution.py
@@ -111,10 +111,11 @@
     ch3 = 3 * ch
     my_rack, my_chip = lax.axis_index("rack"), lax.axis_index("chip")
     me = my_rack * n_chip + my_chip
-    half, n_same = owners // 2, n // 2
+    n_same = n // 2
+    n_own = min(n_same, owners)
+    per = owners // n_own
     core, my_x = lax.rem(my_rack, 2), lax.div(my_rack, 2)
     place = my_x * n_chip + my_chip
-    slot_of_me = core * half + place
     twin = Peer(my_rack + 1 - 2 * core, my_chip, 0)
 
     fetches = [
@@ -137,17 +138,32 @@
             return {"rack": t.rack, "chip": t.chip}
         return {"rack": lax.div(t, n_chip), "chip": lax.rem(t, n_chip)}
 
+    def flipped(x, size):
+        out = []
+        for m in range(size):
+            y = x
+            for bit in (1, 2, 4, 8, 16):
+                if m & bit:
+                    y = y + bit * (1 - 2 * lax.rem(lax.div(x, bit), 2))
+            out.append(y)
+        return out
+
+    def is_power(k):
+        return k & (k - 1) == 0
+
+    few = n <= 32 and is_power(n_rack) and is_power(n_chip)
+    if few:
+        racks, chips = flipped(my_rack, n_rack), flipped(my_chip, n_chip)
+
     def far(k):
-        dr, dc = divmod(k, n_chip)
-        return -min(dc, n_chip - dc) - min(dr, n_rack - dr)
+        r, c = divmod(k, n_chip)
+        return -(c // 2 + c % 2 + r // 2 + 0.3 * (r % 2))
 
     def peers(body):
-        if n <= 32:
+        if few:
             for k in sorted(range(1, n), key=far):
-                dr, dc = divmod(k, n_chip)
-                rack = lax.rem(my_rack + dr, n_rack) if dr else my_rack
-                chip = lax.rem(my_chip + dc, n_chip) if dc else my_chip
-                body(Peer(rack, chip, rack * n_chip + chip))
+                r, c = divmod(k, n_chip)
+                body(Peer(racks[r], chips[c], racks[r] * n_chip + chips[c]))
             return
 
         def step(k, carry):
@@ -188,12 +204,12 @@
         return buf[rnd]
 
     def same_core(body):
-        if n <= 32:
-            for k in sorted(range(1, n_same), key=far):
-                dx, dc = divmod(k, n_chip)
-                x = lax.rem(my_x + dx, n_rack // 2) if dx else my_x
-                chip = lax.rem(my_chip + dc, n_chip) if dc else my_chip
-                body(Peer(x * 2 + core, chip, x * n_chip + chip))
+        if few:
+            for k in sorted(range(n), key=far):
+                r, c = divmod(k, n_chip)
+                if k > 0 and r % 2 == 0:
+                    x = lax.div(racks[r], 2)
+                    body(Peer(racks[r], chips[c], x * n_chip + chips[c]))
             return
 
         def step(k, carry):
@@ -203,23 +219,39 @@
 
         lax.fori_loop(1, n_same, step, 0)
 
+    def on_core(k, body):
+        pl.when(core == k)(body)
+
     def to_twin(src, dst, send, recv):
-        remote(src.at[pl.ds((1 - core) * half, half)], dst, send, recv, twin)
+        on_core(0, lambda: remote(src, dst, send, recv, twin))
+
+    def when_owner(body):
+        on_core(1, body if n_own == n_same else lambda: pl.when(place < n_own)(body))
+
+    def by_role(mine, theirs):
+        if n_own == n_same:
+            mine()
+        else:
+            pl.when(place < n_own)(mine)
+            pl.when(place >= n_own)(theirs)
 
     def send_parts(src, came, both, dst, came_sem, send, recv):
-        landed(came, came_sem)
-        both[...] = src[pl.ds(core * half, half)] + came[...]
-
-        def go(t):
-            def copy():
-                remote(both.at[t.index], dst.at[place], send, recv, t)
-
-            if half == n_same:
-                copy()
-            else:
-                pl.when(t.index < half)(copy)
-
-        same_core(go)
+        def body():
+            landed(came, came_sem)
+            both[...] = src[...] + came[...]
+
+            def go(t):
+                def copy():
+                    remote(both.at[t.index], dst.at[place], send, recv, t)
+
+                if n_own == n_same:
+                    copy()
+                else:
+                    pl.when(t.index < n_own)(copy)
+
+            same_core(go)
+
+        on_core(1, body)
 
     def pass_on(layer):
         send_parts(
@@ -232,19 +264,6 @@
             rs_recv.at[layer],
         )
 
-    def when_owner(body):
-        if half == n_same:
-            body()
-        else:
-            pl.when(place < half)(body)
-
-    def by_role(mine, theirs):
-        if half == n_same:
-            mine()
-        else:
-            pl.when(place < half)(mine)
-            pl.when(place >= half)(theirs)
-
     lane = lax.broadcasted_iota(jnp.int32, (1, 2 * ch), 1)
 
     def add_parts(layer):
@@ -258,31 +277,42 @@
                 rxbuf[at, place] = rxp[at, place]
                 extra = jnp.sum(rxbuf[at], axis=0)
 
-                def mine(row):
-                    even = jnp.sum(jnp.where(lane == 2 * slot_of_me, row, 0.0), axis=1, keepdims=True)
-                    odd = jnp.sum(jnp.where(lane == 2 * slot_of_me + 1, row, 0.0), axis=1, keepdims=True)
+                def mine(row, k):
+                    first = 2 * (k * n_own + place)
+                    even = jnp.sum(jnp.where(lane == first, row, 0.0), axis=1, keepdims=True)
+                    odd = jnp.sum(jnp.where(lane == first + 1, row, 0.0), axis=1, keepdims=True)
                     return jnp.where(lane < ch, even, odd)
 
                 sums = sigmas[layer]
                 inv = pltpu.roll(sq[layer, 0:1, :], ch, axis=1)
                 gain = par[11 + layer : 12 + layer, :]
-                c_dy = mine(sums / entries)
-                c_dx = mine(pltpu.roll(sums, ch, axis=1) / entries)
-                total = total - c_dy * extra[9:18] - c_dx * extra[0:9]
-                total = mine(gain * inv) * total
-            grads[layer, slot_of_me] = total
-            out = grads.at[layer, slot_of_me]
+                window = extra[9 * per : 9 * per + 9]
+                parts = []
+                for k in range(per):
+                    c_dy = mine(sums / entries, k)
+                    c_dx = mine(pltpu.roll(sums, ch, axis=1) / entries, k)
+                    at = slice(9 * k, 9 * k + 9)
+                    part = total[at] - c_dy * window - c_dx * extra[at]
+                    parts.append(mine(gain * inv, k) * part)
+                for k in range(per):
+                    grads[layer, place, 9 * k : 9 * k + 9, :] = parts[k]
+            else:
+                grads[layer, place] = total
+            out = grads.at[layer, place]
             same_core(lambda t: remote(out, out, ag_send.at[layer], ag_recv.at[layer], t))
 
         when_owner(body)
 
     def share(layer):
-        by_role(
-            lambda: landed(grads.at[layer, pl.ds(0, half - 1)], ag_recv.at[layer]),
-            lambda: landed(grads.at[layer, pl.ds(0, half)], ag_recv.at[layer]),
-        )
-        ours = grads.at[layer, pl.ds(core * half, half)]
-        remote(ours, ours, sh_send.at[layer], sh_recv.at[layer], twin)
+        def body():
+            by_role(
+                lambda: landed(grads.at[layer, pl.ds(0, n_own - 1)], ag_recv.at[layer]),
+                lambda: landed(grads.at[layer], ag_recv.at[layer]),
+            )
+            whole = grads.at[layer]
+            remote(whole, whole, sh_send.at[layer], sh_recv.at[layer], twin)
+
+        on_core(1, body)
 
     for f in fetches[0:5]:
         f.wait()
@@ -442,9 +472,11 @@
             wb0s[(4 + k) * ch : (5 + k) * ch, :] = lo
 
     for s in range(sweeps):
+        spot = jnp.broadcast_to(spots[s].astype(F32), (8, pill)).T[:, 0:1]
         for k in range(4):
-            ids = lax.broadcasted_iota(jnp.int32, (plane, pill), 0) + k * plane
-            onehot[s, k * plane : (k + 1) * plane, :] = (ids == spots[s]).astype(F32).astype(BF16)
+            ids = lax.broadcasted_iota(jnp.int32, (pill, plane), 1) + k * plane
+            hit = ids.astype(F32) == spot
+            onehot[s, :, k * plane : (k + 1) * plane] = hit.astype(F32).astype(BF16)
     for s in range(sweeps):
         bm[s] = jnp.max(mx[s], axis=1)
     for f in fetches[9:11]:
@@ -476,7 +508,7 @@
     for s in range(sweeps):
         pillar = jnp.maximum(bm[s] * scale_c + shift_c, 0.0)
         hi, lo = split(pillar)
-        placed = dot(jnp.concatenate([hi, lo], axis=0), onehot[s], NT)
+        placed = dot(jnp.concatenate([hi, lo], axis=0), onehot[s])
         for k in range(4):
             part = placed[:, k * plane : (k + 1) * plane]
             planes[k].append(part[0:ch] + part[ch : 2 * ch])
@@ -533,7 +565,8 @@
             keep(slice(0, ch3), correlate(ref[...], ch3, layer + 1))
 
         def store(t, line):
-            rs[layer, :, t, :] = line
+            for k in range(per):
+                rs[layer, :, 9 * k + t, :] = line[k * n_own : (k + 1) * n_own]
 
         pairs(store)
         to_twin(rs.at[layer], ra.at[layer], ra_send.at[layer], ra_recv.at[layer])
@@ -554,15 +587,19 @@
             window = [both[ch3 + b : ch3 + b + 1] for b in range(3)]
 
         def store(t, line):
-            rx[at, :, t, :] = line
+            for k in range(per):
+                rx[at, :, 9 * k + t, :] = line[k * n_own : (k + 1) * n_own]
 
         pairs(store)
         for b in range(3):
             for a in range(3):
                 one = window[b][:, a * ch : (a + 1) * ch]
                 line = jnp.concatenate([one, one], axis=1)
-                rx[at, :, 9 + 3 * a + b, :] = jnp.broadcast_to(line, (owners, 2 * ch))
+                rx[at, :, 9 * per + 3 * a + b, :] = jnp.broadcast_to(line, (n_own, 2 * ch))
         to_twin(rx.at[at], rxa.at[at], rxa_send.at[at], rxa_recv.at[at])
+
+    def pass_extra(layer):
+        at = LINEAR.index(layer)
         send_parts(
             rx.at[at],
             rxa.at[at],
@@ -594,6 +631,8 @@
         row = jnp.where(lane < ch, row / entries_loc, row)
         send_row(st, layer + 1, row)
         xh[layer] = d
+        if layer - 2 in LINEAR:
+            pass_extra(layer - 2)
         if layer + 1 < LAYERS:
             weights(layer + 1)
         else:
@@ -650,13 +689,13 @@
             send_grad(gs, layer + 1)
         if layer in LINEAR:
             pass_on(layer)
-        if layer + 1 < LAYERS and layer + 1 not in LINEAR:
-            pass_on(layer + 1)
+        if layer == 0:
+            share(LAYERS - 1)
         for done in range(LAYERS - 1, layer, -1):
             if done == layer + (1 if done in LINEAR else 2):
                 add_parts(done)
-        if layer == 0:
-            share(LAYERS - 1)
+        if layer + 1 < LAYERS and layer + 1 not in LINEAR:
+            pass_on(layer + 1)
         row = jnp.sum(wait_row(st, rnd), axis=0)
         sigmas[layer] = row
         norms[0, layer : layer + 1, :] = row[:, ch : 2 * ch]
@@ -678,37 +717,49 @@
         total = None
         for k in range(4):
             hi, lo = split(u0[k * ch : (k + 1) * ch, s * plane : (s + 1) * plane])
-            part = dot(
-                jnp.concatenate([hi, lo], axis=0), onehot[s, k * plane : (k + 1) * plane, :]
-            )
+            both = jnp.concatenate([hi, lo], axis=0)
+            part = dot(both, onehot[s, :, k * plane : (k + 1) * plane], NT)
             total = part if total is None else total + part
         pgrad[s] = total[0:ch] + total[ch : 2 * ch]
     add_parts(0)
 
-    for layer in range(LAYERS - 2, -1, -1):
+    def arrived(layer):
+        on_core(0, lambda: landed(grads.at[layer], sh_recv.at[layer]))
+
+    def unpack(layer):
+        arrived(layer)
+        for t in range(9):
+            for k in range(per):
+                part = grads[layer, :, 9 * k + t, :]
+                out_g[t, k * n_own : (k + 1) * n_own, layer, :] = part
+
+    def sent(ref, sem):
+        by_role(lambda: landed(ref.at[pl.ds(0, n_own - 1)], sem), lambda: landed(ref, sem))
+
+    def drain(layer):
+        on_core(0, lambda: landed(ra.at[layer], ra_send.at[layer]))
+        on_core(1, lambda: sent(rp.at[layer], rs_send.at[layer]))
+        when_owner(lambda: landed(rbuf.at[layer, pl.ds(0, n_same - 1)], ag_send.at[layer]))
+
+    for layer in range(LAYERS - 2, 0, -1):
         share(layer)
-
-    for layer in range(LAYERS - 1, -1, -1):
-        landed(grads.at[layer, pl.ds(0, half)], sh_recv.at[layer])
-        for t in range(9):
-            out_g[t, :, layer, :] = grads[layer, :, t, :]
-
     for rnd in range(2 * LAYERS + 1):
         landed((st0.at[0] if rnd == 0 else st.at[rnd]).at[pl.ds(0, n - 1)], st_send.at[rnd])
-    for layer in range(LAYERS):
-        landed(ra.at[layer], ra_send.at[layer])
-        landed(grads.at[layer, pl.ds(0, half)], sh_send.at[layer])
-        by_role(
-            lambda: landed(rp.at[layer, pl.ds(0, half - 1)], rs_send.at[layer]),
-            lambda: landed(rp.at[layer], rs_send.at[layer]),
-        )
-        when_owner(lambda: landed(rbuf.at[layer, pl.ds(0, n_same - 1)], ag_send.at[layer]))
     for at in range(len(LINEAR)):
-        landed(rxa.at[at], rxa_send.at[at])
-        by_role(
-            lambda: landed(rxp.at[at, pl.ds(0, half - 1)], rx_send.at[at]),
-            lambda: landed(rxp.at[at], rx_send.at[at]),
-        )
+        on_core(0, lambda: landed(rxa.at[at], rxa_send.at[at]))
+        on_core(1, lambda: sent(rxp.at[at], rx_send.at[at]))
+    for layer in range(LAYERS - 1, 0, -1):
+        unpack(layer)
+        drain(layer)
+    share(0)
+    drain(0)
+    unpack(0)
+
+    def shared():
+        for layer in range(LAYERS):
+            landed(grads.at[layer], sh_send.at[layer])
+
+    on_core(1, shared)
 
 
 def write_out(a, b, c, d, a_h, b_h, c_h, d_h, sem):
@@ -740,7 +791,9 @@
     gh, gw = 2 * h2, 2 * w2
     n = n_rack * n_chip
     owners = ch // 2
-    assert n >= owners and n_rack % 2 == 0 and w2 == 128 and 2 * ch == 128
+    n_own = min(n // 2, owners)
+    per = owners // n_own
+    assert owners % n_own == 0 and n_rack % 2 == 0 and w2 == 128 and 2 * ch == 128
     pix = sweeps * h2 * w2
     ch3 = 3 * ch
     dims = (n_rack, n_chip, sweeps, maxp, gh, gw, pill, ch, owners)
@@ -780,10 +833,10 @@
             pltpu.VMEM((LAYERS - 1, 2 * ch3, ch3), BF16),
             pltpu.VMEM((8 * ch, 4 * ch), BF16),
             pltpu.VMEM((2, 4 * ch, pix), BF16),
-            pltpu.VMEM((sweeps, gh * gw, pill), BF16),
+            pltpu.VMEM((sweeps, pill, gh * gw), BF16),
             pltpu.VMEM((32, 128), F32),
             pltpu.VMEM((ch, pix), F32),
-            pltpu.VMEM((LAYERS, owners, 9, 2 * ch), F32),
+            pltpu.VMEM((LAYERS, n_own, 9 * per, 2 * ch), F32),
             pltpu.VMEM((sweeps, ch, pill), F32),
             pltpu.VMEM((sweeps, ch, 8, pill), F32),
             pltpu.VMEM((ch, 8, 128), F32),
@@ -791,14 +844,14 @@
             pltpu.VMEM((LAYERS, ch, pix), F32),
             pltpu.VMEM((1, n, 1, 4 * ch), F32),
             pltpu.VMEM((2 * LAYERS + 1, n, 1, 2 * ch), F32),
-            pltpu.VMEM((LAYERS, owners, 9, 2 * ch), F32),
-            pltpu.VMEM((LAYERS, owners // 2, 9, 2 * ch), F32),
-            pltpu.VMEM((LAYERS, owners // 2, 9, 2 * ch), F32),
-            pltpu.VMEM((LAYERS, n // 2, 9, 2 * ch), F32),
-            pltpu.VMEM((extra, owners, 18, 2 * ch), F32),
-            pltpu.VMEM((extra, owners // 2, 18, 2 * ch), F32),
-            pltpu.VMEM((extra, owners // 2, 18, 2 * ch), F32),
-            pltpu.VMEM((extra, n // 2, 18, 2 * ch), F32),
+            pltpu.VMEM((LAYERS, n_own, 9 * per, 2 * ch), F32),
+            pltpu.VMEM((LAYERS, n_own, 9 * per, 2 * ch), F32),
+            pltpu.VMEM((LAYERS, n_own, 9 * per, 2 * ch), F32),
+            pltpu.VMEM((LAYERS, n // 2, 9 * per, 2 * ch), F32),
+            pltpu.VMEM((extra, n_own, 9 * per + 9, 2 * ch), F32),
+            pltpu.VMEM((extra, n_own, 9 * per + 9, 2 * ch), F32),
+            pltpu.VMEM((extra, n_own, 9 * per + 9, 2 * ch), F32),
+            pltpu.VMEM((extra, n // 2, 9 * per + 9, 2 * ch), F32),
             dma((11,)),
             dma((2 * LAYERS + 1,)),
             dma((2 * LAYERS + 1,)),

time: 67.8 us -> 66.8 us (0.985)
  Pallas kernels: 67 us -> 65.9 us
    pallas_call x1, Pallas kernels: 66 us -> 64.9 us  [per_device(): pl.pallas_call(functools.partial(kernel, dims), out_shape=(pltpu.VMEM((sw...]
where the time goes in v3:
time: 66.8 us; the launch traced here: 66.7 us
  Pallas kernels  65.9 us (99%)
  between operations  0.8 us (1%)
    pallas_call x1, Pallas kernels, per_device(): pl.pallas_call(functools.partial(kernel, dims), out_shape=(pltpu.VMEM((sw...  64.9 us

profile of v3, /device:TPU:0, one launch (start us, length us, event | category | flops | bytes accessed | tf_op | source)
XLA Modules:
  0.0 66.7 jit_solution(7683001932760623403)
XLA Ops:
  0.6 64.9 %shard_map.129 = (f32[2,64,4,128]{3,2,1,0:T(4,128)S(1)}, f32[9,32,4,128]{3,2,1,0:T(4,128)S(1)}, f32[2,4,64]{2,1,0:T(4,128)S(1)}, f32[2,64,256]{2,1,0:T(8,128)S(1)}) custom-call(f32[2,4,32,256]{3,2,1,0:T(8,128)} %points_h.1, s32[2,256]{1,0:T(2,128)} %counts_h.1, s32[2,256]{1,0:T(2,128)} %cells_h.1, f32[9,64]{1,0:T(8,128)} %pw_h.1, f32[1,64]{1,0:T(1,128)} %bitcast.9, ...), custom_call_target="tpu_custom_call" | custom-call | tf_op jit(solution)/shard_map/pallas_call | solution.py:805
  65.6 1.0 %shard_map.130 = (f32[2,64,4,128]{3,2,1,0:T(4,128)}, f32[9,32,4,128]{3,2,1,0:T(4,128)}, f32[2,4,64]{2,1,0:T(4,128)}, f32[2,64,256]{2,1,0:T(8,128)}) custom-call(f32[2,64,4,128]{3,2,1,0:T(4,128)S(1)} %get-tuple-element.12.a, f32[9,32,4,128]{3,2,1,0:T(4,128)S(1)} %get-tuple-element.13.b, f32[2,4,64]{2,1,0:T(4,128)S(1)} %get-tuple-element.14.c, ...), custom_call_target="tpu_custom_call" | custom-call | tf_op jit(solution)/shard_map/pallas_call | solution.py:886

commit v4 on v3

--- a/solution.py
+++ b/solution.py
@@ -388,7 +388,7 @@
         sq[c] = folded
         return carry
 
-    lax.fori_loop(0, ch, one_channel, 0)
+    lax.fori_loop(0, ch, one_channel, 0, unroll=4)
     both = jnp.concatenate([jnp.broadcast_to(m_loc, (ch, 128)), jnp.sum(sq[...], axis=1)], axis=0)
     turned = both.T
     row = jnp.where(lane < ch, turned[0:1, :], jnp.sum(turned, axis=0, keepdims=True))
@@ -426,8 +426,8 @@
             for h in range(2):
                 xs[at, h, a * ch : (a + 1) * ch, :] = down(x[h], d) if d else x[h]
 
-    def stack_cols(ref, step, x):
-        for b in range(3):
+    def stack_cols(ref, step, x, taps=3):
+        for b in range(taps):
             for h, part in enumerate(split(shift(x, 1 - b))):
                 ref[h * step + b * ch : h * step + (b + 1) * ch, :] = part
 
@@ -683,7 +683,7 @@
                     at = s * plane + r * w2
                     feat[s, :, r, :] = act[:, at : at + w2]
         if layer in LINEAR:
-            stack_cols(hs, ch3, gy)
+            stack_cols(hs, ch3, gy, 2 if layer == 0 else 3)
             send_grad(hs.at[0 : 2 * ch3, :], layer)
         if layer + 1 < LAYERS and layer + 1 not in LINEAR:
             send_grad(gs, layer + 1)
@@ -763,7 +763,7 @@
 
 
 def write_out(a, b, c, d, a_h, b_h, c_h, d_h, sem):
-    pairs = [(a, a_h), (b, b_h), (c, c_h), (d, d_h)]
+    pairs = [(b, b_h), (a, a_h), (d, d_h), (c, c_h)]
     copies = [pltpu.make_async_copy(x, y, sem.at[i]) for i, (x, y) in enumerate(pairs)]
     for x in copies:
         x.start()

time: 66.8 us -> 66.2 us (level)
  no operation moved by 1% of the time
where the time goes in v4:
time: 66.2 us; the launch traced here: 66.1 us
  Pallas kernels  65.3 us (99%)
  between operations  0.8 us (1%)
    pallas_call x1, Pallas kernels, per_device(): pl.pallas_call(functools.partial(kernel, dims), out_shape=(pltpu.VMEM((sw...  64.3 us

profile of v4, /device:TPU:0, one launch (start us, length us, event | category | flops | bytes accessed | tf_op | source)
XLA Modules:
  0.0 66.1 jit_solution(13392832157597624685)
XLA Ops:
  0.6 64.3 %shard_map.129 = (f32[2,64,4,128]{3,2,1,0:T(4,128)S(1)}, f32[9,32,4,128]{3,2,1,0:T(4,128)S(1)}, f32[2,4,64]{2,1,0:T(4,128)S(1)}, f32[2,64,256]{2,1,0:T(8,128)S(1)}) custom-call(f32[2,4,32,256]{3,2,1,0:T(8,128)} %points_h.1, s32[2,256]{1,0:T(2,128)} %counts_h.1, s32[2,256]{1,0:T(2,128)} %cells_h.1, f32[9,64]{1,0:T(8,128)} %pw_h.1, f32[1,64]{1,0:T(1,128)} %bitcast.9, ...), custom_call_target="tpu_custom_call" | custom-call | tf_op jit(solution)/shard_map/pallas_call | solution.py:805
  64.9 1.0 %shard_map.130 = (f32[2,64,4,128]{3,2,1,0:T(4,128)}, f32[9,32,4,128]{3,2,1,0:T(4,128)}, f32[2,4,64]{2,1,0:T(4,128)}, f32[2,64,256]{2,1,0:T(8,128)}) custom-call(f32[2,64,4,128]{3,2,1,0:T(4,128)S(1)} %get-tuple-element.12.a, f32[9,32,4,128]{3,2,1,0:T(4,128)S(1)} %get-tuple-element.13.b, f32[2,4,64]{2,1,0:T(4,128)S(1)} %get-tuple-element.14.c, ...), custom_call_target="tpu_custom_call" | custom-call | tf_op jit(solution)/shard_map/pallas_call | solution.py:886

commit v5 on v4

--- a/solution.py
+++ b/solution.py
@@ -388,7 +388,7 @@
         sq[c] = folded
         return carry
 
-    lax.fori_loop(0, ch, one_channel, 0, unroll=4)
+    lax.fori_loop(0, ch, one_channel, 0, unroll=8)
     both = jnp.concatenate([jnp.broadcast_to(m_loc, (ch, 128)), jnp.sum(sq[...], axis=1)], axis=0)
     turned = both.T
     row = jnp.where(lane < ch, turned[0:1, :], jnp.sum(turned, axis=0, keepdims=True))

time: 66.2 us -> 66.1 us (level)
  no operation moved by 1% of the time
where the time goes in v5:
time: 66.1 us; the launch traced here: 66 us
  Pallas kernels  65.2 us (99%)
  between operations  0.8 us (1%)
    pallas_call x1, Pallas kernels, per_device(): pl.pallas_call(functools.partial(kernel, dims), out_shape=(pltpu.VMEM((sw...  64.2 us

profile of v5, /device:TPU:0, one launch (start us, length us, event | category | flops | bytes accessed | tf_op | source)
XLA Modules:
  0.0 66.0 jit_solution(13026182263477273628)
XLA Ops:
  0.6 64.2 %shard_map.129 = (f32[2,64,4,128]{3,2,1,0:T(4,128)S(1)}, f32[9,32,4,128]{3,2,1,0:T(4,128)S(1)}, f32[2,4,64]{2,1,0:T(4,128)S(1)}, f32[2,64,256]{2,1,0:T(8,128)S(1)}) custom-call(f32[2,4,32,256]{3,2,1,0:T(8,128)} %points_h.1, s32[2,256]{1,0:T(2,128)} %counts_h.1, s32[2,256]{1,0:T(2,128)} %cells_h.1, f32[9,64]{1,0:T(8,128)} %pw_h.1, f32[1,64]{1,0:T(1,128)} %bitcast.9, ...), custom_call_target="tpu_custom_call" | custom-call | tf_op jit(solution)/shard_map/pallas_call | solution.py:805
  64.8 1.0 %shard_map.130 = (f32[2,64,4,128]{3,2,1,0:T(4,128)}, f32[9,32,4,128]{3,2,1,0:T(4,128)}, f32[2,4,64]{2,1,0:T(4,128)}, f32[2,64,256]{2,1,0:T(8,128)}) custom-call(f32[2,64,4,128]{3,2,1,0:T(4,128)S(1)} %get-tuple-element.12.a, f32[9,32,4,128]{3,2,1,0:T(4,128)S(1)} %get-tuple-element.13.b, f32[2,4,64]{2,1,0:T(4,128)S(1)} %get-tuple-element.14.c, ...), custom_call_target="tpu_custom_call" | custom-call | tf_op jit(solution)/shard_map/pallas_call | solution.py:886
